TPU v7x, 128 devices: a whole 4x4x4 slice. The times are simulated.
128 devices in a mesh: dp: 1, tp: 2 (over core), sp: 64 (over z, y, x).
Axes of the slice: x: 4, y: 4, z: 4, core: 2. Of those that a mesh axis runs over, the one named last changes fastest.
Arguments:
- hidden: bfloat16 [64, 2048], P('dp')
- seq_lens: int32 [64], P('dp')
- k_cache: bfloat16 [64, 2, 8192, 128], P('dp', 'tp', 'sp')
- v_cache: bfloat16 [64, 2, 8192, 128], P('dp', 'tp', 'sp')
- attn_norm: bfloat16 [2048], replicated
- w_q: bfloat16 [2048, 2048], P(None, 'tp')
- w_k: bfloat16 [2048, 256], P(None, 'tp')
- w_v: bfloat16 [2048, 256], P(None, 'tp')
- w_o: bfloat16 [2048, 2048], P('tp')
- mlp_norm: bfloat16 [2048], replicated
- w_gate: bfloat16 [2048, 11008], P(None, 'tp')
- w_up: bfloat16 [2048, 11008], P(None, 'tp')
- w_down: bfloat16 [11008, 2048], P('tp')
Outputs:
- output 1: bfloat16 [64, 2048], P('dp')
- output 2: bfloat16 [64, 2, 8192, 128], P('dp', 'tp', 'sp')
- output 3: bfloat16 [64, 2, 8192, 128], P('dp', 'tp', 'sp')
All inputs are finite; a program needn't handle non-finite values.
Results may differ from a plain program's by a relative error of at most 0.00376563.
Values sent between devices are 32-bit elements.
A program may use at most 1 GiB of HBM per device.

v0:
```python
import jax
import jax.numpy as jnp
from jax import lax
from jax.sharding import PartitionSpec as P

NORM_EPS = 1e-6
MASK_VALUE = -1e30


def rms_norm(values, gain):
    wide = values.astype(jnp.float32)
    scaled = wide * lax.rsqrt(jnp.mean(wide * wide, axis=-1, keepdims=True) + NORM_EPS)
    return (scaled * gain.astype(jnp.float32)).astype(jnp.bfloat16)


def project(normed, weight):
    return jnp.dot(normed, weight, preferred_element_type=jnp.float32).astype(jnp.bfloat16)


def solution(mesh):
    cache_spec = P('dp', 'tp', 'sp', None)
    row_spec = P('dp', None)
    col_spec = P(None, 'tp')
    inner_spec = P('tp', None)
    gain_spec = P(None)

    def local_step(hidden, seq_lens, k_cache, v_cache, attn_norm, w_q, w_k, w_v, w_o, mlp_norm, w_gate, w_up, w_down):
        batch_rows, groups, block_len, head_dim = k_cache.shape
        repeat = w_q.shape[1] // (groups * head_dim)
        normed = rms_norm(hidden, attn_norm)
        query = project(normed, w_q).reshape(batch_rows, groups, repeat, head_dim)
        k_new = project(normed, w_k).reshape(batch_rows, groups, 1, head_dim)
        v_new = project(normed, w_v).reshape(batch_rows, groups, 1, head_dim)
        positions = lax.axis_index('sp') * block_len + jnp.arange(block_len)
        new_slot = (positions[None, :] == seq_lens[:, None])[:, None, :, None]
        k_out = jnp.where(new_slot, k_new, k_cache)
        v_out = jnp.where(new_slot, v_new, v_cache)
        valid = (positions[None, :] <= seq_lens[:, None])[:, None, None, :]
        scores = jnp.einsum('bgrd,bgsd->bgrs', query, k_out, preferred_element_type=jnp.float32) * head_dim ** -0.5
        scores = jnp.where(valid, scores, MASK_VALUE)
        global_max = lax.pmax(jnp.max(scores, axis=-1, keepdims=True), 'sp')
        weights = jnp.where(valid, jnp.exp(scores - global_max), 0.0)
        local_sum = jnp.sum(weights, axis=-1, keepdims=True)
        local_mix = jnp.einsum('bgrs,bgsd->bgrd', weights.astype(jnp.bfloat16), v_out, preferred_element_type=jnp.float32)
        merged = lax.psum(jnp.concatenate([local_mix, local_sum], axis=-1), 'sp')
        attended = (merged[..., :head_dim] / merged[..., head_dim:]).astype(jnp.bfloat16).reshape(batch_rows, groups * repeat * head_dim)
        proj_part = jnp.dot(attended, w_o, preferred_element_type=jnp.float32)
        mid_hidden = (hidden.astype(jnp.float32) + lax.psum(proj_part, 'tp')).astype(jnp.bfloat16)
        normed_mid = rms_norm(mid_hidden, mlp_norm)
        gate_proj = jnp.dot(normed_mid, w_gate, preferred_element_type=jnp.float32)
        up_proj = jnp.dot(normed_mid, w_up, preferred_element_type=jnp.float32)
        activated = (jax.nn.silu(gate_proj) * up_proj).astype(jnp.bfloat16)
        down_part = jnp.dot(activated, w_down, preferred_element_type=jnp.float32)
        hidden_out = (mid_hidden.astype(jnp.float32) + lax.psum(down_part, 'tp')).astype(jnp.bfloat16)
        return hidden_out, k_out, v_out

    return jax.shard_map(local_step, mesh=mesh, in_specs=(row_spec, P('dp'), cache_spec, cache_spec, gain_spec, col_spec, col_spec, col_spec, inner_spec, gain_spec, col_spec, col_spec, inner_spec), out_specs=(row_spec, cache_spec, cache_spec), check_vma=False)
```

profile of v0, /device:TPU:1, one launch (start us, length us, event | category | flops | bytes accessed | tf_op | source)
XLA Modules:
  0.0 587.6 jit_solution(10322090472626846512)
XLA Ops:
  7.3 1.2 fusion.21
  8.4 0.7 convert_element_type.46
  9.1 1.2 convolution_convert_fusion.2
  10.4 1.4 convolution_convert_fusion.1
  11.8 3.2 fusion.19
  15.3 1.4 broadcast_select_fusion
  16.7 1.3 copy-done.3
  18.0 1.3 fusion.49
  19.3 296.4 %pmax.7 = f32[64,8]{1,0:T(8,128)S(1)} all-reduce(f32[64,8]{1,0:T(8,128)S(1)} %get-tuple-element.9), channel_id=1, replica_groups=mesh['dp'=1,'tp'=2,'sp'=64] {'sp'}, use_global_device_ids=true, to_apply=%region_2.3 | all-reduce | flops 512 | bytes 4096 | tf_op jit(solution)/shard_map/pmax | solution.py:41
  315.6 0.2 fusion.30
  315.9 0.7 fusion.16
  316.6 0.5 copy.20
  317.0 0.9 pad_maximum_fusion
  318.0 175.1 %all-reduce.4.cloned.1.call-done = f32[64,1,8,129]{3,2,0,1:T(8,128)} async-done(((f32[64,1,8,129]{3,2,0,1:T(8,128)}), f32[64,1,8,129]{3,2,0,1:T(8,128)}) %all-reduce.4.cloned.1.call-update) | async-done | bytes 264208 | tf_op jit(solution)/shard_map/psum | solution.py:45
  493.1 1.0 slice.9
  494.1 0.4 copy.25
  494.5 1.1 fusion.29
  495.6 3.8 fusion.33
  499.6 24.4 %all-reduce.6.cloned.1.call-done = f32[64,2048]{1,0:T(8,128)} async-done(((f32[64,2048]{1,0:T(8,128)}), f32[64,2048]{1,0:T(8,128)}) %all-reduce.6.cloned.1.call-update) | async-done | bytes 524304 | tf_op jit(solution)/shard_map/psum | solution.py:48
  523.9 1.2 fusion.25
  525.2 9.6 %fusion.41 = f32[64,5504]{1,0:T(8,128)S(1)} fusion(bf16[2048,5504]{1,0:T(8,128)(2,1)} %param.23, bf16[64,2048]{1,0:T(8,128)(2,1)S(1)} %get-tuple-element.4, f32[2048]{0:T(1024)S(1)} %convert_element_type.55, f32[64]{0:T(128)S(1)} %add_rsqrt_fusion), kind=kOutput, calls=%fused_computation.47 | convolution fusion | flops 1443364864 | bytes 24224000 | tf_op jit(solution)/shard_map/dot_general | solution.py:50
  534.8 18.9 %fusion.5 = f32[64,2048]{1,0:T(8,128)} fusion(bf16[5504,2048]{1,0:T(8,128)(2,1)} %param.25, bf16[2048,5504]{1,0:T(8,128)(2,1)} %param.24, f32[64,5504]{1,0:T(8,128)S(1)} %fusion.41, bf16[64,2048]{1,0:T(8,128)(2,1)S(1)} %get-tuple-element.4, f32[2048]{0:T(1024)S(1)} %convert_element_type.55, f32[64]{0:T(128)S(1)} %add_rsqrt_fusion), kind=kOutput, calls=%fused_computation.8 | convolution fusion | flops 2888318976 | bytes 47292672 | tf_op jit(solution)/shard_map/dot_general | solution.py:53
  553.8 25.5 %all-reduce.8.cloned.1.call-done = f32[64,2048]{1,0:T(8,128)} async-done(((f32[64,2048]{1,0:T(8,128)}), f32[64,2048]{1,0:T(8,128)}) %all-reduce.8.cloned.1.call-update) | async-done | bytes 524304 | tf_op jit(solution)/shard_map/psum | solution.py:54
  579.3 1.8 fusion.28
  (29 shorter events, 0.4 us)
Async XLA Ops:
  7.2 2.0 copy-start
  7.2 4.6 copy-start.4
  7.2 485.9 %all-reduce.4.cloned.1.call-start = ((), (), s32[]{:S(2)}) async-start(), calls=%async_computation | async-start | bytes 1048576 | tf_op jit(solution)/shard_map/psum | solution.py:45
  11.8 3.3 copy-start.8
  11.8 3.4 copy-start.5
  11.8 3.5 copy-start.6
  16.7 1.3 copy-start.3
  16.7 299.9 %copy-start.2 = (bf16[64,1,128,128]{3,2,1,0:T(8,128)(2,1)}, bf16[64,1,128,128]{3,2,1,0:T(8,128)(2,1)S(1)}, u32[]{:S(2)}) copy-start(bf16[64,1,128,128]{3,2,1,0:T(8,128)(2,1)S(1)} %get-tuple-element.5) | copy-start | bytes 6291460
  317.9 206.0 %all-reduce.6.cloned.1.call-start = ((), (), s32[]{:S(2)}) async-start(), calls=%async_computation.1 | async-start | bytes 1048576 | tf_op jit(solution)/shard_map/psum | solution.py:48
  495.6 3.9 copy-start.7
  499.5 79.8 %all-reduce.8.cloned.1.call-start = ((), (), s32[]{:S(2)}) async-start(), calls=%async_computation.2 | async-start | bytes 1048576 | tf_op jit(solution)/shard_map/psum | solution.py:54
  534.8 46.2 %copy-start.1 = (bf16[2048,128]{1,0:T(8,128)(2,1)S(1)}, bf16[2048,128]{1,0:T(8,128)(2,1)}, u32[]{:S(2)}) copy-start(bf16[2048,128]{1,0:T(8,128)(2,1)} %param.19) | copy-start | bytes 1572868
Sparse Core Ops, SparseCore 0:
  318.0 175.0 all-reduce.3
  499.6 24.2 all-reduce.5
  553.9 25.3 all-reduce.7
where the time goes:
time: 588 us
  blocking collectives  296 us (50%)
  waiting for transfers between devices  225 us (38%)
  matrix products  40.2 us (7%)
  between operations  14 us (2%)
  other arithmetic  8.54 us (1%)
    pmax x1, blocking collectives, local_step(): global_max = lax.pmax(jnp.max(scores, axis=-1, keepdims=True), 'sp')  296 us
    psum x1, waiting for transfers between devices, local_step(): merged = lax.psum(jnp.concatenate([local_mix, local_sum], axis=-1), 'sp')  175 us
    psum x1, waiting for transfers between devices, local_step(): lax.psum(down_part, 'tp')  25.5 us
    psum x1, waiting for transfers between devices, local_step(): lax.psum(proj_part, 'tp')  24.4 us
    dot_general x1, matrix products, local_step(): down_part = jnp.dot(activated, w_down, preferred_element_type=jnp.float32)  18.9 us
  transfers between devices with their start and end apart: 3, of which 3 were waited for; matrix products, arithmetic and copies ran while one was open for 0% of the time, Pallas kernels for 0%

commit v1 on v0

v1 whole, which is shorter than its diff:
```python
import functools

import jax
import jax.numpy as jnp
from jax import lax
from jax.experimental import pallas as pl
from jax.experimental.pallas import tpu as pltpu
from jax.sharding import PartitionSpec as P

NORM_EPS = 1e-6
MESH = pl.DeviceIdType.MESH
F32 = jnp.float32
BF16 = jnp.bfloat16
SEQ_CHUNKS = 4
Q_COLS = 256
FF_COLS = 512
FF_SLOTS = 6
OUT_COLS = 512


def rms_norm(wide, gain):
    scaled = wide * lax.rsqrt(jnp.mean(wide * wide, axis=-1, keepdims=True) + NORM_EPS)
    return (scaled * gain).astype(BF16)


def dot(a, b):
    return jnp.dot(a, b, preferred_element_type=F32)


def attention_kernel(lens_ref, hidden_ref, gain_ref, wq_hbm, wk_hbm, wv_hbm, k_hbm, v_hbm,
                     k_out, v_out, mix_ref, stats_ref,
                     wq, wk, wv, kbuf, vbuf, query, k_new, v_new, scores, probs, w_sem, q_sem, k_sem, v_sem, ko_sem, vo_sem):
    rows, block_len, head_dim = kbuf.shape
    repeat = mix_ref.shape[1]
    per = rows // SEQ_CHUNKS
    q_chunks = wq_hbm.shape[1] // Q_COLS
    scale = head_dim ** -0.5
    base = lax.axis_index('sp') * block_len

    def q_copy(c):
        cols = pl.ds(c * Q_COLS, Q_COLS)
        return pltpu.make_async_copy(wq_hbm.at[:, cols], wq.at[:, cols], q_sem.at[c])

    def cache_copy(hbm, buf, sems, c):
        part = pl.ds(c * per, per)
        return pltpu.make_async_copy(hbm.at[part], buf.at[part], sems.at[c])

    def out_copy(buf, hbm, sems, c):
        part = pl.ds(c * per, per)
        return pltpu.make_async_copy(buf.at[part], hbm.at[part], sems.at[c])

    k_weights = pltpu.make_async_copy(wk_hbm, wk, w_sem.at[0])
    v_weights = pltpu.make_async_copy(wv_hbm, wv, w_sem.at[1])
    k_weights.start()
    v_weights.start()
    for c in range(q_chunks):
        q_copy(c).start()
    for c in range(SEQ_CHUNKS):
        cache_copy(k_hbm, kbuf, k_sem, c).start()
    for c in range(SEQ_CHUNKS):
        cache_copy(v_hbm, vbuf, v_sem, c).start()

    normed = rms_norm(hidden_ref[...].astype(F32), gain_ref[...].astype(F32))
    k_weights.wait()
    k_new[...] = dot(normed, wk[...]).astype(BF16).astype(F32)
    v_weights.wait()
    v_new[...] = dot(normed, wv[...]).astype(BF16).astype(F32)
    for c in range(q_chunks):
        q_copy(c).wait()
        part = dot(normed, wq[:, c * Q_COLS:(c + 1) * Q_COLS]).astype(BF16).astype(F32)
        for h in range(Q_COLS // head_dim):
            query[:, c * (Q_COLS // head_dim) + h, :] = part[:, h * head_dim:(h + 1) * head_dim]

    lanes = lax.broadcasted_iota(jnp.int32, (repeat, block_len), 1)
    tile = lax.broadcasted_iota(jnp.int32, (16, head_dim), 0)

    def insert(buf, new, b, slot):
        start = pl.multiple_of(jnp.clip(slot, 0, block_len - 1) // 16 * 16, 16)
        old = buf[b, pl.ds(start, 16), :]
        fresh = jnp.broadcast_to(new[pl.ds(b, 1), :], (16, head_dim)).astype(BF16)
        buf[b, pl.ds(start, 16), :] = jnp.where(tile == slot - start, fresh, old)

    def score_chunk(c, carry):
        cache_copy(k_hbm, kbuf, k_sem, c).wait()
        for i in range(per):
            b = c * per + i
            insert(kbuf, k_new, b, lens_ref[b] - base)
        out_copy(kbuf, k_out, ko_sem, c).start()
        for i in range(per):
            b = c * per + i
            raw = lax.dot_general(query[b].astype(BF16), kbuf[b], (((1,), (1,)), ((), ())), preferred_element_type=F32)
            scores[b] = jnp.where(lanes <= lens_ref[b] - base, raw * scale, -jnp.inf)
        return carry

    lax.fori_loop(0, SEQ_CHUNKS, score_chunk, 0)

    pairs = lax.broadcasted_iota(jnp.int32, (128, block_len), 1)
    group = 128 // repeat
    half = group // 2

    def soft_chunk(c, carry):
        s = scores[pl.ds(c * group, group)].reshape(128, block_len)
        top = jnp.max(s, axis=-1, keepdims=True)
        p = jnp.where(s > -jnp.inf, jnp.exp(s - top), 0.0)
        total = jnp.sum(p, axis=-1, keepdims=True)
        probs[pl.ds(c * group, group)] = p.reshape(group, repeat, block_len)
        flipped = jnp.where(pairs == 0, top, jnp.where(pairs == 1, total, 0.0)).T
        m_row, l_row = flipped[0:1], flipped[1:2]
        low = lax.broadcasted_iota(jnp.int32, (1, 128), 1) < half * repeat
        stats_ref[2 * c] = jnp.where(low, m_row, pltpu.roll(l_row, half * repeat, 1))
        stats_ref[2 * c + 1] = jnp.where(low, pltpu.roll(m_row, half * repeat, 1), l_row)
        return carry

    lax.fori_loop(0, rows // group, soft_chunk, 0)

    def mix_chunk(c, carry):
        cache_copy(v_hbm, vbuf, v_sem, c).wait()
        for i in range(per):
            b = c * per + i
            insert(vbuf, v_new, b, lens_ref[b] - base)
        out_copy(vbuf, v_out, vo_sem, c).start()
        for i in range(per):
            b = c * per + i
            mix_ref[b] = dot(probs[b].astype(BF16), vbuf[b])
        return carry

    lax.fori_loop(0, SEQ_CHUNKS, mix_chunk, 0)
    for c in range(SEQ_CHUNKS):
        out_copy(kbuf, k_out, ko_sem, c).wait()
        out_copy(vbuf, v_out, vo_sem, c).wait()


def attention(hidden, seq_lens, gain, w_q, w_k, w_v, k_cache, v_cache):
    rows, block_len, head_dim = k_cache.shape
    repeat = w_q.shape[1] // head_dim
    whole = pl.BlockSpec(memory_space=pltpu.VMEM)
    raw = pl.BlockSpec(memory_space=pl.ANY)
    return pl.pallas_call(
        attention_kernel,
        name='attention',
        out_shape=(
            jax.ShapeDtypeStruct(k_cache.shape, BF16),
            jax.ShapeDtypeStruct(v_cache.shape, BF16),
            jax.ShapeDtypeStruct((rows, repeat, head_dim), F32),
            jax.ShapeDtypeStruct((2 * rows * repeat // 128, 1, 128), F32),
        ),
        in_specs=[pl.BlockSpec(memory_space=pltpu.SMEM), whole, whole, raw, raw, raw, raw, raw],
        out_specs=(raw, raw, whole, whole),
        scratch_shapes=[
            pltpu.VMEM(w_q.shape, BF16),
            pltpu.VMEM(w_k.shape, BF16),
            pltpu.VMEM(w_v.shape, BF16),
            pltpu.VMEM(k_cache.shape, BF16),
            pltpu.VMEM(v_cache.shape, BF16),
            pltpu.VMEM((rows, repeat, head_dim), F32),
            pltpu.VMEM((rows, head_dim), F32),
            pltpu.VMEM((rows, head_dim), F32),
            pltpu.VMEM((rows, repeat, block_len), F32),
            pltpu.VMEM((rows, repeat, block_len), F32),
            pltpu.SemaphoreType.DMA((2,)),
            pltpu.SemaphoreType.DMA((w_q.shape[1] // Q_COLS,)),
            pltpu.SemaphoreType.DMA((SEQ_CHUNKS,)),
            pltpu.SemaphoreType.DMA((SEQ_CHUNKS,)),
            pltpu.SemaphoreType.DMA((SEQ_CHUNKS,)),
            pltpu.SemaphoreType.DMA((SEQ_CHUNKS,)),
        ],
        compiler_params=pltpu.CompilerParams(vmem_limit_bytes=24 << 20),
    )(seq_lens, hidden, gain, w_q, w_k, w_v, k_cache, v_cache)


def merge_kernel(hidden_ref, mix_ref, stats_ref, gain_ref, wo_hbm, wg_hbm, wu_hbm, wd_hbm, out_ref,
                 got_mix, got_stats, flipped, own, gathered, wo, wg, wu, wd, sent, other, mid_ref, normed_ref, act, sent2, other2,
                 mix_send, mix_recv, st_send, st_recv, own_send, own_recv, o_send, o_recv, d_send, d_recv,
                 wo_sem, g_sem, u_sem, wd_sem):
    rows, repeat, head_dim = mix_ref.shape
    n = rows
    me = lax.axis_index('sp')
    partner = 1 - lax.axis_index('tp')
    inner = wg_hbm.shape[1]
    full = inner // FF_COLS
    tail = inner - full * FF_COLS
    outs = wo_hbm.shape[1] // OUT_COLS
    per_row = 128 // (2 * repeat)

    barrier = pltpu.get_barrier_semaphore()

    def greet(d, carry):
        pl.semaphore_signal(barrier, inc=1, device_id={'sp': lax.rem(me + d, n)}, device_id_type=MESH)
        return carry

    lax.fori_loop(1, n, greet, 0)
    pl.semaphore_signal(barrier, inc=1, device_id={'tp': partner}, device_id_type=MESH)

    wo_copy = pltpu.make_async_copy(wo_hbm, wo, wo_sem)
    wo_copy.start()

    def ff_copies(i, width=FF_COLS):
        slot = lax.rem(i, FF_SLOTS) if not isinstance(i, int) else i % FF_SLOTS
        start = i * FF_COLS if isinstance(i, int) else pl.multiple_of(i * FF_COLS, FF_COLS)
        cols = pl.ds(start, width)
        return (
            pltpu.make_async_copy(wg_hbm.at[:, cols], wg.at[slot, :, pl.ds(0, width)], g_sem.at[slot]),
            pltpu.make_async_copy(wu_hbm.at[:, cols], wu.at[slot, :, pl.ds(0, width)], u_sem.at[slot]),
        )

    def down_copy(c):
        return pltpu.make_async_copy(wd_hbm.at[:, pl.ds(pl.multiple_of(c * OUT_COLS, OUT_COLS), OUT_COLS)], wd.at[c], wd_sem.at[c])

    for i in range(FF_SLOTS):
        for copy in ff_copies(i):
            copy.start()
    for c in range(outs):
        down_copy(c).start()

    pl.semaphore_wait(barrier, n)

    def send_part(d, carry):
        peer = lax.rem(me + d, n)
        pltpu.make_async_remote_copy(mix_ref.at[peer], got_mix.at[me], mix_send, mix_recv, device_id={'sp': peer}, device_id_type=MESH).start()
        pltpu.make_async_remote_copy(stats_ref.at[peer // per_row], got_stats.at[me], st_send, st_recv, device_id={'sp': peer}, device_id_type=MESH).start()
        return carry

    lax.fori_loop(1, n, send_part, 0)
    got_mix[me] = mix_ref[me]
    got_stats[me] = stats_ref[me // per_row]

    def bulk(ref, send, recv):
        span = ref.at[pl.ds(0, n - 1)]
        return pltpu.make_async_remote_copy(span, span, send, recv, device_id={'tp': partner}, device_id_type=MESH)

    bulk(got_stats, st_send, st_recv).wait_recv()
    flipped[...] = got_stats[:, 0, :].T
    first = pl.multiple_of(lax.rem(me, per_row) * repeat, repeat)
    tops = flipped[pl.ds(first, repeat), :]
    totals = flipped[pl.ds(pl.multiple_of(per_row * repeat + first, repeat), repeat), :]
    factor = jnp.exp(tops - jnp.max(tops, axis=-1, keepdims=True))
    total = jnp.sum(factor * totals, axis=-1, keepdims=True)
    bulk(got_mix, mix_send, mix_recv).wait_recv()
    lanes = 4
    sums = [factor[:, s:s + 1] * got_mix[s] for s in range(lanes)]
    for s in range(lanes, n):
        sums[s % lanes] = sums[s % lanes] + factor[:, s:s + 1] * got_mix[s]
    mixed = (sums[0] + sums[1]) + (sums[2] + sums[3])
    row = (mixed / total).astype(BF16).astype(F32)
    own[...] = row
    gathered[me] = row

    def send_own(d, carry):
        pltpu.make_async_remote_copy(own, gathered.at[me], own_send, own_recv, device_id={'sp': lax.rem(me + d, n)}, device_id_type=MESH).start()
        return carry

    lax.fori_loop(1, n, send_own, 0)
    wo_copy.wait()
    bulk(gathered, own_send, own_recv).wait_recv()
    attended = jnp.concatenate([gathered[:, h, :] for h in range(repeat)], axis=-1).astype(BF16)

    def exchange(mine, theirs, send, recv, c):
        return pltpu.make_async_remote_copy(mine.at[c], theirs.at[c], send.at[c], recv.at[c], device_id={'tp': partner}, device_id_type=MESH)

    for c in range(outs):
        sent[c] = dot(attended, wo[:, c * OUT_COLS:(c + 1) * OUT_COLS])
        exchange(sent, other, o_send, o_recv, c).start()
    square = 0.0
    for c in range(outs):
        exchange(sent, other, o_send, o_recv, c).wait_recv()
        cols = slice(c * OUT_COLS, (c + 1) * OUT_COLS)
        mid = (hidden_ref[:, cols].astype(F32) + (sent[c] + other[c])).astype(BF16)
        mid_ref[:, cols] = mid
    normed_ref[...] = rms_norm(mid_ref[...].astype(F32), gain_ref[...].astype(F32))

    def inner_step(slot, start, width):
        normed = normed_ref[...]
        gate = dot(normed, wg[slot, :, :width])
        up = dot(normed, wu[slot, :, :width])
        act[:, pl.ds(start, width)] = (jax.nn.silu(gate) * up).astype(BF16)

    def ff_step(i, carry):
        for copy in ff_copies(i):
            copy.wait()
        slot = lax.rem(i, FF_SLOTS)
        inner_step(slot, pl.multiple_of(i * FF_COLS, FF_COLS), FF_COLS)

        @pl.when(i + FF_SLOTS < full)
        def _():
            for copy in ff_copies(i + FF_SLOTS):
                copy.start()

        if tail:
            @pl.when(i + FF_SLOTS == full)
            def _():
                for copy in ff_copies(full, tail):
                    copy.start()
        return carry

    lax.fori_loop(0, full, ff_step, 0)
    if tail:
        for copy in ff_copies(full, tail):
            copy.wait()
        inner_step(full % FF_SLOTS, full * FF_COLS, tail)

    def down_step(c, carry):
        down_copy(c).wait()
        sent2[c] = dot(act[...], wd[c])
        exchange(sent2, other2, d_send, d_recv, c).start()
        return carry

    lax.fori_loop(0, outs, down_step, 0)
    for c in range(outs):
        exchange(sent2, other2, d_send, d_recv, c).wait_recv()
        cols = slice(c * OUT_COLS, (c + 1) * OUT_COLS)
        out_ref[:, cols] = (mid_ref[:, cols].astype(F32) + (sent2[c] + other2[c])).astype(BF16)

    bulk(got_mix, mix_send, mix_recv).wait_send()
    bulk(got_stats, st_send, st_recv).wait_send()
    bulk(gathered, own_send, own_recv).wait_send()
    for c in range(outs):
        exchange(sent, other, o_send, o_recv, c).wait_send()
        exchange(sent2, other2, d_send, d_recv, c).wait_send()


def merge(hidden, mix, stats, gain, w_o, w_gate, w_up, w_down):
    rows, repeat, head_dim = mix.shape
    width = w_o.shape[1]
    inner = w_gate.shape[1]
    outs = width // OUT_COLS
    whole = pl.BlockSpec(memory_space=pltpu.VMEM)
    raw = pl.BlockSpec(memory_space=pl.ANY)
    dma = pltpu.SemaphoreType.DMA
    return pl.pallas_call(
        merge_kernel,
        name='merge',
        out_shape=jax.ShapeDtypeStruct(hidden.shape, BF16),
        in_specs=[whole, whole, whole, whole, raw, raw, raw, raw],
        out_specs=whole,
        scratch_shapes=[
            pltpu.VMEM(mix.shape, F32),
            pltpu.VMEM((rows, 1, 128), F32),
            pltpu.VMEM((128, rows), F32),
            pltpu.VMEM((repeat, head_dim), F32),
            pltpu.VMEM(mix.shape, F32),
            pltpu.VMEM(w_o.shape, BF16),
            pltpu.VMEM((FF_SLOTS, width, FF_COLS), BF16),
            pltpu.VMEM((FF_SLOTS, width, FF_COLS), BF16),
            pltpu.VMEM((outs, inner, OUT_COLS), BF16),
            pltpu.VMEM((outs, rows, OUT_COLS), F32),
            pltpu.VMEM((outs, rows, OUT_COLS), F32),
            pltpu.VMEM((rows, width), BF16),
            pltpu.VMEM((rows, width), BF16),
            pltpu.VMEM((rows, inner), BF16),
            pltpu.VMEM((outs, rows, OUT_COLS), F32),
            pltpu.VMEM((outs, rows, OUT_COLS), F32),
            dma, dma, dma, dma, dma, dma,
            dma((outs,)), dma((outs,)), dma((outs,)), dma((outs,)),
            dma, dma((FF_SLOTS,)), dma((FF_SLOTS,)), dma((outs,)),
        ],
        compiler_params=pltpu.CompilerParams(collective_id=0, has_side_effects=True, vmem_limit_bytes=63 << 20),
    )(hidden, mix, stats, gain, w_o, w_gate, w_up, w_down)


def solution(mesh):
    cache_spec = P('dp', 'tp', 'sp', None)
    row_spec = P('dp', None)
    col_spec = P(None, 'tp')
    inner_spec = P('tp', None)
    gain_spec = P(None)

    def local_step(hidden, seq_lens, k_cache, v_cache, attn_norm, w_q, w_k, w_v, w_o, mlp_norm, w_gate, w_up, w_down):
        shape = k_cache.shape
        flat = (shape[0] * shape[1], shape[2], shape[3])
        k_out, v_out, mix, stats = attention(hidden, seq_lens, attn_norm[None, :], w_q, w_k, w_v, k_cache.reshape(flat), v_cache.reshape(flat))
        hidden_out = merge(hidden, mix, stats, mlp_norm[None, :], w_o, w_gate, w_up, w_down)
        return hidden_out, k_out.reshape(shape), v_out.reshape(shape)

    return jax.shard_map(local_step, mesh=mesh, in_specs=(row_spec, P('dp'), cache_spec, cache_spec, gain_spec, col_spec, col_spec, col_spec, inner_spec, gain_spec, col_spec, col_spec, inner_spec), out_specs=(row_spec, cache_spec, cache_spec), check_vma=False)
```

time: 588 us -> 68.2 us (0.12)
  blocking collectives: 296 us -> 0 us
  waiting for transfers between devices: 225 us -> 0 us
  Pallas kernels: 0 us -> 53 us
  matrix products: 40.2 us -> 0 us
  between operations: 14 us -> 0.66 us
  local copies, waits for them, and re-layouts: 3.32 us -> 14 us
  other arithmetic: 8.54 us -> 0 us
    pmax x1 -> x0, blocking collectives: 296 us -> none  [local_step(): global_max = lax.pmax(jnp.max(scores, axis=-1, keepdims=True), 'sp')]
    psum x3 -> x0, waiting for transfers between devices: 225 us -> none  [the longest x1 175 us: local_step(): merged = lax.psum(jnp.concatenate([local_mix, local_sum], axis=-1), 'sp')]
    pallas_call x0 -> x2, Pallas kernels: none -> 53 us  [the longest x1 43.9 us: merge(): pl.pallas_call(merge_kernel, name='merge', out_shape=jax.ShapeDtypeStruct...]
    dot_general x8 -> x0, matrix products: 40.2 us -> none  [the longest x1 18.9 us: local_step(): down_part = jnp.dot(activated, w_down, preferred_element_type=jnp.float32)]
    unnamed x19, local copies, waits for them, and re-layouts: 1.47 us -> 12 us
  transfers between devices with their start and end apart: 3 -> 0, of which waited for: 3 -> 0; matrix products, arithmetic and copies ran while one was open for 0% -> 0% of each run, Pallas kernels for 0% -> 0%
where the time goes in v1:
time: 68.2 us; the launch traced here: 67.7 us
  Pallas kernels  53 us (78%)
  local copies, waits for them, and re-layouts  14 us (21%)
    pallas_call x1, Pallas kernels, merge(): pl.pallas_call(merge_kernel, name='merge', out_shape=jax.ShapeDtypeStruct...  43.9 us
    unnamed x19, local copies, waits for them, and re-layouts  12 us
    pallas_call x1, Pallas kernels, attention(): pl.pallas_call(attention_kernel, name='attention', out_shape=(jax.ShapeDt...  9.13 us

profile of v1, /device:TPU:1, one launch (start us, length us, event | category | flops | bytes accessed | tf_op | source)
XLA Modules:
  0.0 67.7 jit_solution(11404715960216469520)
XLA Ops:
  0.6 0.7 %broadcast_in_dim.6.gain_ref = bf16[1,2048]{1,0:T(2,128)(2,1)S(1)} reshape(bf16[2048]{0:T(1024)(128)(2,1)} %param.17) | data formatting | bytes 8192 | tf_op jit(solution)/shard_map/broadcast_in_dim | solution.py:370
  1.3 1.3 %broadcast_in_dim.7.gain_ref = bf16[1,2048]{1,0:T(2,128)(2,1)} reshape(bf16[2048]{0:T(1024)(128)(2,1)} %param.22) | data formatting | bytes 8192 | tf_op jit(solution)/shard_map/broadcast_in_dim | solution.py:371
  2.6 0.0 copy-start
  2.6 2.2 %copy-done = bf16[2048,1024]{1,0:T(8,128)(2,1)S(1)} copy-done((bf16[2048,1024]{1,0:T(8,128)(2,1)S(1)}, bf16[2048,1024]{1,0:T(8,128)(2,1)}, u32[]{:S(2)}) %copy-start) | copy-done | bytes 4194328
  4.8 0.0 copy-start.1
  4.8 1.6 %copy-done.1 = bf16[64,1,128,128]{3,2,1,0:T(8,128)(2,1)S(1)} copy-done((bf16[64,1,128,128]{3,2,1,0:T(8,128)(2,1)S(1)}, bf16[64,1,128,128]{3,2,1,0:T(8,128)(2,1)}, u32[]{:S(2)}) %copy-start.1) | copy-done | bytes 2097176
  6.4 0.0 copy-start.2
  6.4 1.6 %copy-done.2 = bf16[64,1,128,128]{3,2,1,0:T(8,128)(2,1)S(1)} copy-done((bf16[64,1,128,128]{3,2,1,0:T(8,128)(2,1)S(1)}, bf16[64,1,128,128]{3,2,1,0:T(8,128)(2,1)}, u32[]{:S(2)}) %copy-start.2) | copy-done | bytes 2097176
  8.0 0.0 copy-start.3
  8.0 0.9 %copy-done.3 = bf16[64,2048]{1,0:T(8,128)(2,1)S(1)} copy-done((bf16[64,2048]{1,0:T(8,128)(2,1)S(1)}, bf16[64,2048]{1,0:T(8,128)(2,1)}, u32[]{:S(2)}) %copy-start.3) | copy-done | bytes 262168
  8.9 0.0 copy-start.4
  8.9 1.0 %copy-done.4 = bf16[2048,128]{1,0:T(8,128)(2,1)S(1)} copy-done((bf16[2048,128]{1,0:T(8,128)(2,1)S(1)}, bf16[2048,128]{1,0:T(8,128)(2,1)}, u32[]{:S(2)}) %copy-start.4) | copy-done | bytes 524312
  10.0 0.0 copy-start.5
  10.0 1.0 %copy-done.5 = bf16[2048,128]{1,0:T(8,128)(2,1)S(1)} copy-done((bf16[2048,128]{1,0:T(8,128)(2,1)S(1)}, bf16[2048,128]{1,0:T(8,128)(2,1)}, u32[]{:S(2)}) %copy-start.5) | copy-done | bytes 524312
  11.0 0.0 copy-start.8
  11.0 0.7 copy-done.8
  11.7 9.1 %attention.1 = (bf16[64,128,128]{2,1,0:T(8,128)(2,1)}, bf16[64,128,128]{2,1,0:T(8,128)(2,1)}, f32[64,8,128]{2,1,0:T(8,128)S(1)}, f32[8,1,128]{2,1,0:T(1,128)S(1)}) custom-call(s32[64]{0:T(128)S(1)} %copy-done.8, bf16[64,2048]{1,0:T(8,128)(2,1)S(1)} %copy-done.3, bf16[1,2048]{1,0:T(2,128)(2,1)S(1)} %broadcast_in_dim.6.gain_ref, ...), custom_call_target="tpu_custom_call" | custom-call | tf_op jit(solution)/shard_map/attention/pallas_call | solution.py:138
  20.8 0.0 copy-start.6
  20.8 0.7 %copy-done.6 = f32[64,8,128]{2,1,0:T(8,128)} copy-done((f32[64,8,128]{2,1,0:T(8,128)}, f32[64,8,128]{2,1,0:T(8,128)S(1)}, u32[]{:S(2)}) %copy-start.6) | copy-done | bytes 262168
  21.5 0.0 copy-start.7
  21.5 0.6 copy-done.7
  22.1 43.9 %merge.1 = bf16[64,2048]{1,0:T(8,128)(2,1)} custom-call(bf16[64,2048]{1,0:T(8,128)(2,1)} %hidden_ref.3, f32[64,8,128]{2,1,0:T(8,128)} %copy-done.6, f32[8,1,128]{2,1,0:T(1,128)} %copy-done.7, bf16[1,2048]{1,0:T(2,128)(2,1)} %broadcast_in_dim.7.gain_ref, bf16[1024,2048]{1,0:T(8,128)(2,1)} %wo_hbm.1, bf16[2048,5504]{1,0:T(8,128)(2,1)} %wg_hbm.1, ...), custom_call_target="tpu_custom_call" | custom-call | tf_op jit(solution)/shard_map/merge/pallas_call | solution.py:329
  66.0 1.7 %copy.19 = bf16[64,2048]{1,0:T(8,128)(2,1)} copy(bf16[64,2048]{1,0:T(8,128)(2,1)} %merge.1) | data formatting | bytes 524288
Async XLA Ops:
  2.6 2.2 %copy-start = (bf16[2048,1024]{1,0:T(8,128)(2,1)S(1)}, bf16[2048,1024]{1,0:T(8,128)(2,1)}, u32[]{:S(2)}) copy-start(bf16[2048,1024]{1,0:T(8,128)(2,1)} %wq_hbm.1) | copy-start | bytes 12582916
  4.8 1.6 %copy-start.1 = (bf16[64,1,128,128]{3,2,1,0:T(8,128)(2,1)S(1)}, bf16[64,1,128,128]{3,2,1,0:T(8,128)(2,1)}, u32[]{:S(2)}) copy-start(bf16[64,1,128,128]{3,2,1,0:T(8,128)(2,1)} %param.15) | copy-start | bytes 6291460
  6.4 1.6 %copy-start.2 = (bf16[64,1,128,128]{3,2,1,0:T(8,128)(2,1)S(1)}, bf16[64,1,128,128]{3,2,1,0:T(8,128)(2,1)}, u32[]{:S(2)}) copy-start(bf16[64,1,128,128]{3,2,1,0:T(8,128)(2,1)} %param.16) | copy-start | bytes 6291460
  8.0 0.9 %copy-start.3 = (bf16[64,2048]{1,0:T(8,128)(2,1)S(1)}, bf16[64,2048]{1,0:T(8,128)(2,1)}, u32[]{:S(2)}) copy-start(bf16[64,2048]{1,0:T(8,128)(2,1)} %hidden_ref.3) | copy-start | bytes 786436
  8.9 1.0 %copy-start.4 = (bf16[2048,128]{1,0:T(8,128)(2,1)S(1)}, bf16[2048,128]{1,0:T(8,128)(2,1)}, u32[]{:S(2)}) copy-start(bf16[2048,128]{1,0:T(8,128)(2,1)} %wk_hbm.1) | copy-start | bytes 1572868
  10.0 1.0 %copy-start.5 = (bf16[2048,128]{1,0:T(8,128)(2,1)S(1)}, bf16[2048,128]{1,0:T(8,128)(2,1)}, u32[]{:S(2)}) copy-start(bf16[2048,128]{1,0:T(8,128)(2,1)} %wv_hbm.1) | copy-start | bytes 1572868
  11.0 0.7 copy-start.8
  20.8 0.7 %copy-start.6 = (f32[64,8,128]{2,1,0:T(8,128)}, f32[64,8,128]{2,1,0:T(8,128)S(1)}, u32[]{:S(2)}) copy-start(f32[64,8,128]{2,1,0:T(8,128)S(1)} %get-tuple-element.7.mix_ref) | copy-start | bytes 786436
  21.5 0.6 copy-start.7

commit v2 on v1

--- a/solution.py
+++ b/solution.py
@@ -27,9 +27,13 @@
     return jnp.dot(a, b, preferred_element_type=F32)
 
 
-def attention_kernel(lens_ref, hidden_ref, gain_ref, wq_hbm, wk_hbm, wv_hbm, k_hbm, v_hbm,
+def stay(*arrays, space=pltpu.HBM):
+    return [pltpu.with_memory_space_constraint(x, space) for x in arrays]
+
+
+def attention_kernel(lens_hbm, hidden_hbm, gain_hbm, wq_hbm, wk_hbm, wv_hbm, k_hbm, v_hbm,
                      k_out, v_out, mix_ref, stats_ref,
-                     wq, wk, wv, kbuf, vbuf, query, k_new, v_new, scores, probs, w_sem, q_sem, k_sem, v_sem, ko_sem, vo_sem):
+                     lens_ref, hidden_ref, gain_ref, wq, wk, wv, kbuf, vbuf, query, k_new, v_new, scores, probs, small_sem, w_sem, q_sem, k_sem, v_sem, ko_sem, vo_sem):
     rows, block_len, head_dim = kbuf.shape
     repeat = mix_ref.shape[1]
     per = rows // SEQ_CHUNKS
@@ -49,6 +53,10 @@
         part = pl.ds(c * per, per)
         return pltpu.make_async_copy(buf.at[part], hbm.at[part], sems.at[c])
 
+    small = [pltpu.make_async_copy(src, dst, small_sem.at[i]) for i, (src, dst) in enumerate(
+        ((hidden_hbm, hidden_ref), (gain_hbm, gain_ref), (lens_hbm, lens_ref)))]
+    for copy in small:
+        copy.start()
     k_weights = pltpu.make_async_copy(wk_hbm, wk, w_sem.at[0])
     v_weights = pltpu.make_async_copy(wv_hbm, wv, w_sem.at[1])
     k_weights.start()
@@ -60,7 +68,9 @@
     for c in range(SEQ_CHUNKS):
         cache_copy(v_hbm, vbuf, v_sem, c).start()
 
-    normed = rms_norm(hidden_ref[...].astype(F32), gain_ref[...].astype(F32))
+    for copy in small:
+        copy.wait()
+    normed = rms_norm(hidden_ref[...].astype(F32), gain_ref[...].astype(F32)[None, :])
     k_weights.wait()
     k_new[...] = dot(normed, wk[...]).astype(BF16).astype(F32)
     v_weights.wait()
@@ -134,7 +144,7 @@
     rows, block_len, head_dim = k_cache.shape
     repeat = w_q.shape[1] // head_dim
     whole = pl.BlockSpec(memory_space=pltpu.VMEM)
-    raw = pl.BlockSpec(memory_space=pl.ANY)
+    raw = pl.BlockSpec(memory_space=pltpu.HBM)
     return pl.pallas_call(
         attention_kernel,
         name='attention',
@@ -144,9 +154,12 @@
             jax.ShapeDtypeStruct((rows, repeat, head_dim), F32),
             jax.ShapeDtypeStruct((2 * rows * repeat // 128, 1, 128), F32),
         ),
-        in_specs=[pl.BlockSpec(memory_space=pltpu.SMEM), whole, whole, raw, raw, raw, raw, raw],
+        in_specs=[raw] * 8,
         out_specs=(raw, raw, whole, whole),
         scratch_shapes=[
+            pltpu.SMEM(seq_lens.shape, jnp.int32),
+            pltpu.VMEM(hidden.shape, BF16),
+            pltpu.VMEM(gain.shape, BF16),
             pltpu.VMEM(w_q.shape, BF16),
             pltpu.VMEM(w_k.shape, BF16),
             pltpu.VMEM(w_v.shape, BF16),
@@ -157,6 +170,7 @@
             pltpu.VMEM((rows, head_dim), F32),
             pltpu.VMEM((rows, repeat, block_len), F32),
             pltpu.VMEM((rows, repeat, block_len), F32),
+            pltpu.SemaphoreType.DMA((3,)),
             pltpu.SemaphoreType.DMA((2,)),
             pltpu.SemaphoreType.DMA((w_q.shape[1] // Q_COLS,)),
             pltpu.SemaphoreType.DMA((SEQ_CHUNKS,)),
@@ -164,14 +178,14 @@
             pltpu.SemaphoreType.DMA((SEQ_CHUNKS,)),
             pltpu.SemaphoreType.DMA((SEQ_CHUNKS,)),
         ],
-        compiler_params=pltpu.CompilerParams(vmem_limit_bytes=24 << 20),
-    )(seq_lens, hidden, gain, w_q, w_k, w_v, k_cache, v_cache)
-
-
-def merge_kernel(hidden_ref, mix_ref, stats_ref, gain_ref, wo_hbm, wg_hbm, wu_hbm, wd_hbm, out_ref,
-                 got_mix, got_stats, flipped, own, gathered, wo, wg, wu, wd, sent, other, mid_ref, normed_ref, act, sent2, other2,
+        compiler_params=pltpu.CompilerParams(vmem_limit_bytes=30 << 20),
+    )(*stay(seq_lens, hidden, gain, w_q, w_k, w_v, k_cache, v_cache))
+
+
+def merge_kernel(hidden_hbm, mix_ref, stats_ref, gain_hbm, wo_hbm, wg_hbm, wu_hbm, wd_hbm, out_ref,
+                 hidden_ref, gain_ref, got_mix, got_stats, flipped, own, gathered, wo, wg, wu, wd, sent, other, mid_ref, normed_ref, act, sent2, other2,
                  mix_send, mix_recv, st_send, st_recv, own_send, own_recv, o_send, o_recv, d_send, d_recv,
-                 wo_sem, g_sem, u_sem, wd_sem):
+                 small_sem, wo_sem, g_sem, u_sem, wd_sem):
     rows, repeat, head_dim = mix_ref.shape
     n = rows
     me = lax.axis_index('sp')
@@ -191,6 +205,10 @@
     lax.fori_loop(1, n, greet, 0)
     pl.semaphore_signal(barrier, inc=1, device_id={'tp': partner}, device_id_type=MESH)
 
+    small = [pltpu.make_async_copy(src, dst, small_sem.at[i]) for i, (src, dst) in enumerate(
+        ((hidden_hbm, hidden_ref), (gain_hbm, gain_ref)))]
+    for copy in small:
+        copy.start()
     wo_copy = pltpu.make_async_copy(wo_hbm, wo, wo_sem)
     wo_copy.start()
 
@@ -260,13 +278,14 @@
     for c in range(outs):
         sent[c] = dot(attended, wo[:, c * OUT_COLS:(c + 1) * OUT_COLS])
         exchange(sent, other, o_send, o_recv, c).start()
-    square = 0.0
+    for copy in small:
+        copy.wait()
     for c in range(outs):
         exchange(sent, other, o_send, o_recv, c).wait_recv()
         cols = slice(c * OUT_COLS, (c + 1) * OUT_COLS)
         mid = (hidden_ref[:, cols].astype(F32) + (sent[c] + other[c])).astype(BF16)
         mid_ref[:, cols] = mid
-    normed_ref[...] = rms_norm(mid_ref[...].astype(F32), gain_ref[...].astype(F32))
+    normed_ref[...] = rms_norm(mid_ref[...].astype(F32), gain_ref[...].astype(F32)[None, :])
 
     def inner_step(slot, start, width):
         normed = normed_ref[...]
@@ -324,15 +343,17 @@
     inner = w_gate.shape[1]
     outs = width // OUT_COLS
     whole = pl.BlockSpec(memory_space=pltpu.VMEM)
-    raw = pl.BlockSpec(memory_space=pl.ANY)
+    raw = pl.BlockSpec(memory_space=pltpu.HBM)
     dma = pltpu.SemaphoreType.DMA
     return pl.pallas_call(
         merge_kernel,
         name='merge',
-        out_shape=jax.ShapeDtypeStruct(hidden.shape, BF16),
-        in_specs=[whole, whole, whole, whole, raw, raw, raw, raw],
+        out_shape=pltpu.VMEM(hidden.shape, BF16),
+        in_specs=[raw, whole, whole, raw, raw, raw, raw, raw],
         out_specs=whole,
         scratch_shapes=[
+            pltpu.VMEM(hidden.shape, BF16),
+            pltpu.VMEM(gain.shape, BF16),
             pltpu.VMEM(mix.shape, F32),
             pltpu.VMEM((rows, 1, 128), F32),
             pltpu.VMEM((128, rows), F32),
@@ -351,10 +372,10 @@
             pltpu.VMEM((outs, rows, OUT_COLS), F32),
             dma, dma, dma, dma, dma, dma,
             dma((outs,)), dma((outs,)), dma((outs,)), dma((outs,)),
-            dma, dma((FF_SLOTS,)), dma((FF_SLOTS,)), dma((outs,)),
+            dma((2,)), dma, dma((FF_SLOTS,)), dma((FF_SLOTS,)), dma((outs,)),
         ],
-        compiler_params=pltpu.CompilerParams(collective_id=0, has_side_effects=True, vmem_limit_bytes=63 << 20),
-    )(hidden, mix, stats, gain, w_o, w_gate, w_up, w_down)
+        compiler_params=pltpu.CompilerParams(collective_id=0, has_side_effects=True, vmem_limit_bytes=58 << 20),
+    )(*stay(hidden), *stay(mix, stats, space=pltpu.VMEM), *stay(gain, w_o, w_gate, w_up, w_down))
 
 
 def solution(mesh):
@@ -367,8 +388,8 @@
     def local_step(hidden, seq_lens, k_cache, v_cache, attn_norm, w_q, w_k, w_v, w_o, mlp_norm, w_gate, w_up, w_down):
         shape = k_cache.shape
         flat = (shape[0] * shape[1], shape[2], shape[3])
-        k_out, v_out, mix, stats = attention(hidden, seq_lens, attn_norm[None, :], w_q, w_k, w_v, k_cache.reshape(flat), v_cache.reshape(flat))
-        hidden_out = merge(hidden, mix, stats, mlp_norm[None, :], w_o, w_gate, w_up, w_down)
+        k_out, v_out, mix, stats = attention(hidden, seq_lens, attn_norm, w_q, w_k, w_v, k_cache.reshape(flat), v_cache.reshape(flat))
+        hidden_out = merge(hidden, mix, stats, mlp_norm, w_o, w_gate, w_up, w_down)
         return hidden_out, k_out.reshape(shape), v_out.reshape(shape)
 
     return jax.shard_map(local_step, mesh=mesh, in_specs=(row_spec, P('dp'), cache_spec, cache_spec, gain_spec, col_spec, col_spec, col_spec, inner_spec, gain_spec, col_spec, col_spec, inner_spec), out_specs=(row_spec, cache_spec, cache_spec), check_vma=False)

time: 68.2 us -> 54.5 us (0.80)
  local copies, waits for them, and re-layouts: 14 us -> 0.71 us
    unnamed x19 -> x1, local copies, waits for them, and re-layouts: 12 us -> 0.71 us
    broadcast_in_dim x2 -> x0, local copies, waits for them, and re-layouts: 1.99 us -> none  [the longest x1 1.29 us: local_step(): mlp_norm[None, :]]
    pallas_call x1, Pallas kernels: 9.13 us -> 10.8 us  [attention(): pl.pallas_call(attention_kernel, name='attention', out_shape=(jax.ShapeDt...]
    pallas_call x1, Pallas kernels: 43.9 us -> 42.3 us  [merge(): pl.pallas_call(merge_kernel, name='merge', out_shape=pltpu.VMEM(hidden.sh...]
where the time goes in v2:
time: 54.5 us; the launch traced here: 54.4 us
  Pallas kernels  53.1 us (97%)
  local copies, waits for them, and re-layouts  0.71 us (1%)
  between operations  0.65 us (1%)
    pallas_call x1, Pallas kernels, merge(): pl.pallas_call(merge_kernel, name='merge', out_shape=pltpu.VMEM(hidden.sh...  42.3 us
    pallas_call x1, Pallas kernels, attention(): pl.pallas_call(attention_kernel, name='attention', out_shape=(jax.ShapeDt...  10.8 us

profile of v2, /device:TPU:1, one launch (start us, length us, event | category | flops | bytes accessed | tf_op | source)
XLA Modules:
  0.0 54.4 jit_solution(7827383824584653588)
XLA Ops:
  0.6 10.8 %attention.1 = (bf16[64,128,128]{2,1,0:T(8,128)(2,1)}, bf16[64,128,128]{2,1,0:T(8,128)(2,1)}, f32[64,8,128]{2,1,0:T(8,128)S(1)}, f32[8,1,128]{2,1,0:T(1,128)S(1)}) custom-call(s32[64]{0:T(128)} %lens_hbm.1, bf16[64,2048]{1,0:T(8,128)(2,1)} %hidden_hbm.3, bf16[2048]{0:T(1024)(128)(2,1)} %gain_hbm.2, bf16[2048,1024]{1,0:T(8,128)(2,1)} %wq_hbm.1, ...), custom_call_target="tpu_custom_call" | custom-call | tf_op jit(solution)/shard_map/attention/pallas_call | solution.py:148
  11.4 42.3 %merge.1 = bf16[64,2048]{1,0:T(8,128)(2,1)S(1)} custom-call(bf16[64,2048]{1,0:T(8,128)(2,1)} %hidden_hbm.3, f32[64,8,128]{2,1,0:T(8,128)S(1)} %get-tuple-element.7.mix_ref, f32[8,1,128]{2,1,0:T(1,128)S(1)} %get-tuple-element.8.stats_ref, bf16[2048]{0:T(1024)(128)(2,1)} %gain_hbm.3, bf16[1024,2048]{1,0:T(8,128)(2,1)} %wo_hbm.1, bf16[2048,5504]{1,0:T(8,128)(2,1)} %wg_hbm.1, ...), custom_call_target="tpu_custom_call" | custom-call | tf_op jit(solution)/shard_map/merge/pallas_call | solution.py:348
  53.7 0.7 %copy.19 = bf16[64,2048]{1,0:T(8,128)(2,1)} copy(bf16[64,2048]{1,0:T(8,128)(2,1)S(1)} %merge.1) | data formatting | bytes 524288

commit v3 on v2

--- a/solution.py
+++ b/solution.py
@@ -1,4 +1,4 @@
-import functools
+import itertools
 
 import jax
 import jax.numpy as jnp
@@ -12,6 +12,7 @@
 F32 = jnp.float32
 BF16 = jnp.bfloat16
 SEQ_CHUNKS = 4
+PAD_ROWS = 128
 Q_COLS = 256
 FF_COLS = 512
 FF_SLOTS = 6
@@ -102,7 +103,8 @@
             scores[b] = jnp.where(lanes <= lens_ref[b] - base, raw * scale, -jnp.inf)
         return carry
 
-    lax.fori_loop(0, SEQ_CHUNKS, score_chunk, 0)
+    for c in range(SEQ_CHUNKS):
+        score_chunk(c, 0)
 
     pairs = lax.broadcasted_iota(jnp.int32, (128, block_len), 1)
     group = 128 // repeat
@@ -121,7 +123,8 @@
         stats_ref[2 * c + 1] = jnp.where(low, pltpu.roll(m_row, half * repeat, 1), l_row)
         return carry
 
-    lax.fori_loop(0, rows // group, soft_chunk, 0)
+    for c in range(rows // group):
+        soft_chunk(c, 0)
 
     def mix_chunk(c, carry):
         cache_copy(v_hbm, vbuf, v_sem, c).wait()
@@ -134,7 +137,8 @@
             mix_ref[b] = dot(probs[b].astype(BF16), vbuf[b])
         return carry
 
-    lax.fori_loop(0, SEQ_CHUNKS, mix_chunk, 0)
+    for c in range(SEQ_CHUNKS):
+        mix_chunk(c, 0)
     for c in range(SEQ_CHUNKS):
         out_copy(kbuf, k_out, ko_sem, c).wait()
         out_copy(vbuf, v_out, vo_sem, c).wait()
@@ -232,13 +236,20 @@
 
     pl.semaphore_wait(barrier, n)
 
-    def send_part(d, carry):
-        peer = lax.rem(me + d, n)
+    side = round(n ** (1 / 3))
+    xs = [lax.rem(lax.rem(me, side) + d, side) for d in range(side)]
+    ys = [lax.rem(lax.rem(me // side, side) + d, side) * side for d in range(side)]
+    zs = [lax.rem(me // (side * side) + d, side) * (side * side) for d in range(side)]
+    hops = lambda o: sum(min(d, side - d) for d in o)
+    offsets = sorted(itertools.product(range(side), repeat=3), key=hops, reverse=True)[:-1]
+    peers = [xs[a] + ys[b] + zs[c] for a, b, c in offsets]
+
+    def send_part(peer):
         pltpu.make_async_remote_copy(mix_ref.at[peer], got_mix.at[me], mix_send, mix_recv, device_id={'sp': peer}, device_id_type=MESH).start()
         pltpu.make_async_remote_copy(stats_ref.at[peer // per_row], got_stats.at[me], st_send, st_recv, device_id={'sp': peer}, device_id_type=MESH).start()
-        return carry
-
-    lax.fori_loop(1, n, send_part, 0)
+
+    for peer in peers:
+        send_part(peer)
     got_mix[me] = mix_ref[me]
     got_stats[me] = stats_ref[me // per_row]
 
@@ -263,11 +274,11 @@
     own[...] = row
     gathered[me] = row
 
-    def send_own(d, carry):
-        pltpu.make_async_remote_copy(own, gathered.at[me], own_send, own_recv, device_id={'sp': lax.rem(me + d, n)}, device_id_type=MESH).start()
-        return carry
-
-    lax.fori_loop(1, n, send_own, 0)
+    def send_own(peer):
+        pltpu.make_async_remote_copy(own, gathered.at[me], own_send, own_recv, device_id={'sp': peer}, device_id_type=MESH).start()
+
+    for peer in peers:
+        send_own(peer)
     wo_copy.wait()
     bulk(gathered, own_send, own_recv).wait_recv()
     attended = jnp.concatenate([gathered[:, h, :] for h in range(repeat)], axis=-1).astype(BF16)
@@ -285,13 +296,16 @@
         cols = slice(c * OUT_COLS, (c + 1) * OUT_COLS)
         mid = (hidden_ref[:, cols].astype(F32) + (sent[c] + other[c])).astype(BF16)
         mid_ref[:, cols] = mid
-    normed_ref[...] = rms_norm(mid_ref[...].astype(F32), gain_ref[...].astype(F32)[None, :])
+    normed_ref[0:rows] = rms_norm(mid_ref[...].astype(F32), gain_ref[...].astype(F32)[None, :])
+
+    normed_ref[rows:] = jnp.zeros((PAD_ROWS - rows, normed_ref.shape[1]), BF16)
+    act[rows:] = jnp.zeros((PAD_ROWS - rows, act.shape[1]), BF16)
 
     def inner_step(slot, start, width):
         normed = normed_ref[...]
-        gate = dot(normed, wg[slot, :, :width])
-        up = dot(normed, wu[slot, :, :width])
-        act[:, pl.ds(start, width)] = (jax.nn.silu(gate) * up).astype(BF16)
+        gate = dot(normed, wg[slot, :, :width])[:rows]
+        up = dot(normed, wu[slot, :, :width])[:rows]
+        act[0:rows, pl.ds(start, width)] = (jax.nn.silu(gate) * up).astype(BF16)
 
     def ff_step(i, carry):
         for copy in ff_copies(i):
@@ -319,7 +333,7 @@
 
     def down_step(c, carry):
         down_copy(c).wait()
-        sent2[c] = dot(act[...], wd[c])
+        sent2[c] = dot(act[...], wd[c])[:rows]
         exchange(sent2, other2, d_send, d_recv, c).start()
         return carry
 
@@ -366,8 +380,8 @@
             pltpu.VMEM((outs, rows, OUT_COLS), F32),
             pltpu.VMEM((outs, rows, OUT_COLS), F32),
             pltpu.VMEM((rows, width), BF16),
-            pltpu.VMEM((rows, width), BF16),
-            pltpu.VMEM((rows, inner), BF16),
+            pltpu.VMEM((PAD_ROWS, width), BF16),
+            pltpu.VMEM((PAD_ROWS, inner), BF16),
             pltpu.VMEM((outs, rows, OUT_COLS), F32),
             pltpu.VMEM((outs, rows, OUT_COLS), F32),
             dma, dma, dma, dma, dma, dma,

time: 54.5 us -> 51.4 us (0.943)
  Pallas kernels: 53.1 us -> 50 us
    pallas_call x1, Pallas kernels: 42.3 us -> 40.1 us  [merge(): pl.pallas_call(merge_kernel, name='merge', out_shape=pltpu.VMEM(hidden.sh...]
    pallas_call x1, Pallas kernels: 10.8 us -> 9.89 us  [attention(): pl.pallas_call(attention_kernel, name='attention', out_shape=(jax.ShapeDt...]
where the time goes in v3:
time: 51.4 us; the launch traced here: 51.3 us
  Pallas kernels  50 us (97%)
  local copies, waits for them, and re-layouts  0.71 us (1%)
  between operations  0.65 us (1%)
    pallas_call x1, Pallas kernels, merge(): pl.pallas_call(merge_kernel, name='merge', out_shape=pltpu.VMEM(hidden.sh...  40.1 us
    pallas_call x1, Pallas kernels, attention(): pl.pallas_call(attention_kernel, name='attention', out_shape=(jax.ShapeDt...  9.89 us

profile of v3, /device:TPU:1, one launch (start us, length us, event | category | flops | bytes accessed | tf_op | source)
XLA Modules:
  0.0 51.3 jit_solution(5441996096948217739)
XLA Ops:
  0.6 9.9 %attention.1 = (bf16[64,128,128]{2,1,0:T(8,128)(2,1)}, bf16[64,128,128]{2,1,0:T(8,128)(2,1)}, f32[64,8,128]{2,1,0:T(8,128)S(1)}, f32[8,1,128]{2,1,0:T(1,128)S(1)}) custom-call(s32[64]{0:T(128)} %lens_hbm.1, bf16[64,2048]{1,0:T(8,128)(2,1)} %hidden_hbm.3, bf16[2048]{0:T(1024)(128)(2,1)} %gain_hbm.2, bf16[2048,1024]{1,0:T(8,128)(2,1)} %wq_hbm.1, ...), custom_call_target="tpu_custom_call" | custom-call | tf_op jit(solution)/shard_map/attention/pallas_call | solution.py:152
  10.5 40.1 %merge.1 = bf16[64,2048]{1,0:T(8,128)(2,1)S(1)} custom-call(bf16[64,2048]{1,0:T(8,128)(2,1)} %hidden_hbm.3, f32[64,8,128]{2,1,0:T(8,128)S(1)} %get-tuple-element.7.mix_ref, f32[8,1,128]{2,1,0:T(1,128)S(1)} %get-tuple-element.8.stats_ref, bf16[2048]{0:T(1024)(128)(2,1)} %gain_hbm.3, bf16[1024,2048]{1,0:T(8,128)(2,1)} %wo_hbm.1, bf16[2048,5504]{1,0:T(8,128)(2,1)} %wg_hbm.1, ...), custom_call_target="tpu_custom_call" | custom-call | tf_op jit(solution)/shard_map/merge/pallas_call | solution.py:362
  50.6 0.7 %copy.19 = bf16[64,2048]{1,0:T(8,128)(2,1)} copy(bf16[64,2048]{1,0:T(8,128)(2,1)S(1)} %merge.1) | data formatting | bytes 524288

commit v4 on v0

v4 whole, which is shorter than its diff:
```python
import itertools

import jax
import jax.numpy as jnp
from jax import lax
from jax.experimental import pallas as pl
from jax.experimental.pallas import tpu as pltpu
from jax.sharding import PartitionSpec as P

NORM_EPS = 1e-6
MESH = pl.DeviceIdType.MESH
F32 = jnp.float32
BF16 = jnp.bfloat16
SEQ_CHUNKS = 4
PAD_ROWS = 128
FF_COLS = 512
FF_SLOTS = 6
OUT_COLS = 512


def rms_norm(wide, gain):
    scaled = wide * lax.rsqrt(jnp.mean(wide * wide, axis=-1, keepdims=True) + NORM_EPS)
    return (scaled * gain).astype(BF16)


def dot(a, b):
    return jnp.dot(a, b, preferred_element_type=F32)


def stay(*arrays, space=pltpu.HBM):
    return [pltpu.with_memory_space_constraint(x, space) for x in arrays]


def layer_kernel(lens_hbm, hidden_hbm, gain_hbm, gain2_hbm, wq_hbm, wk_hbm, wv_hbm, k_hbm, v_hbm, wo_hbm, wg_hbm, wu_hbm, wd_hbm,
                 out_ref, kbuf, vbuf,
                 lens_ref, hidden_ref, gain_ref, gain2_ref, wkv, query, new_rows, new_scores, scores, probs, mix_ref, stats_ref,
                 got_mix, got_stats, flipped, own, gathered, wo, wg, wu, wd, sent, other, mid_ref, normed_ref, act, sent2, other2,
                 mix_send, mix_recv, st_send, st_recv, own_send, own_recv, o_send, o_recv, d_send, d_recv,
                 small_sem, w_sem, q_sem, k_sem, v_sem, wo_sem, g_sem, u_sem, wd_sem):
    rows, block_len, head_dim = kbuf.shape
    repeat = mix_ref.shape[1]
    n = rows
    me = lax.axis_index('sp')
    partner = 1 - lax.axis_index('tp')
    base = me * block_len
    scale = head_dim ** -0.5
    per = rows // SEQ_CHUNKS
    inner = wg_hbm.shape[1]
    full = inner // FF_COLS
    tail = inner - full * FF_COLS
    outs = wo_hbm.shape[1] // OUT_COLS
    per_row = 128 // (2 * repeat)

    small = [pltpu.make_async_copy(src, dst, small_sem.at[i]) for i, (src, dst) in enumerate(
        ((hidden_hbm, hidden_ref), (gain_hbm, gain_ref), (lens_hbm, lens_ref), (gain2_hbm, gain2_ref)))]
    for copy in small:
        copy.start()

    kv_copies = [pltpu.make_async_copy(src, wkv.at[:, pl.ds(i * head_dim, head_dim)], w_sem.at[i]) for i, src in enumerate((wk_hbm, wv_hbm))]
    for copy in kv_copies:
        copy.start()
    last = FF_SLOTS - 1
    halves = (wg.at[last], wu.at[last])
    q_copies = [pltpu.make_async_copy(wq_hbm.at[:, pl.ds(i * FF_COLS, FF_COLS)], half, q_sem.at[i]) for i, half in enumerate(halves)]
    for copy in q_copies:
        copy.start()

    def cache_copy(hbm, buf, sems, c):
        part = pl.ds(c * per, per)
        return pltpu.make_async_copy(hbm.at[part], buf.at[part], sems.at[c])

    for c in range(SEQ_CHUNKS):
        cache_copy(k_hbm, kbuf, k_sem, c).start()
    for c in range(SEQ_CHUNKS):
        cache_copy(v_hbm, vbuf, v_sem, c).start()

    barrier = pltpu.get_barrier_semaphore()
    side = round(n ** (1 / 3))
    xs = [lax.rem(lax.rem(me, side) + d, side) for d in range(side)]
    ys = [lax.rem(lax.rem(me // side, side) + d, side) * side for d in range(side)]
    zs = [lax.rem(me // (side * side) + d, side) * (side * side) for d in range(side)]
    hops = lambda o: sum(min(d, side - d) for d in o)
    offsets = sorted(itertools.product(range(side), repeat=3), key=hops, reverse=True)[:-1]
    peers = [xs[a] + ys[b] + zs[c] for a, b, c in offsets]
    for peer in peers:
        pl.semaphore_signal(barrier, inc=1, device_id={'sp': peer}, device_id_type=MESH)
    pl.semaphore_signal(barrier, inc=1, device_id={'tp': partner}, device_id_type=MESH)

    wo_copy = pltpu.make_async_copy(wo_hbm, wo, wo_sem)
    wo_copy.start()

    def ff_copies(i, width=FF_COLS):
        slot = lax.rem(i, FF_SLOTS) if not isinstance(i, int) else i % FF_SLOTS
        start = i * FF_COLS if isinstance(i, int) else pl.multiple_of(i * FF_COLS, FF_COLS)
        cols = pl.ds(start, width)
        return (
            pltpu.make_async_copy(wg_hbm.at[:, cols], wg.at[slot, :, pl.ds(0, width)], g_sem.at[slot]),
            pltpu.make_async_copy(wu_hbm.at[:, cols], wu.at[slot, :, pl.ds(0, width)], u_sem.at[slot]),
        )

    def down_copy(c):
        return pltpu.make_async_copy(wd_hbm.at[:, pl.ds(pl.multiple_of(c * OUT_COLS, OUT_COLS), OUT_COLS)], wd.at[c], wd_sem.at[c])

    for i in range(last):
        for copy in ff_copies(i):
            copy.start()

    normed_ref[rows:] = jnp.zeros((PAD_ROWS - rows, normed_ref.shape[1]), BF16)
    act[rows:] = jnp.zeros((PAD_ROWS - rows, act.shape[1]), BF16)
    for copy in small[:3]:
        copy.wait()
    normed_ref[0:rows] = rms_norm(hidden_ref[...].astype(F32), gain_ref[...].astype(F32)[None, :])
    for copy in kv_copies:
        copy.wait()
    new_rows[...] = dot(normed_ref[...], wkv[...])[:rows].astype(BF16).astype(F32)
    per_half = FF_COLS // head_dim
    for i, half in enumerate(halves):
        q_copies[i].wait()
        part = dot(normed_ref[...], half[...])[:rows].astype(BF16).astype(F32)
        for h in range(per_half):
            query[:, i * per_half + h, :] = part[:, h * head_dim:(h + 1) * head_dim]
    for copy in ff_copies(last):
        copy.start()
    for c in range(outs):
        down_copy(c).start()

    group = 128 // repeat
    for c in range(rows // group):
        part = slice(c * group, (c + 1) * group)
        hit = jnp.sum(query[part] * new_rows[part, :head_dim][:, None, :], axis=-1, keepdims=True) * scale
        new_scores[part] = jnp.broadcast_to(hit, (group, repeat, block_len))

    lanes = lax.broadcasted_iota(jnp.int32, (repeat, block_len), 1)

    def score_chunk(c):
        cache_copy(k_hbm, kbuf, k_sem, c).wait()
        for b in range(c * per, (c + 1) * per):
            slot = lens_ref[b] - base
            raw = lax.dot_general(query[b].astype(BF16), kbuf[b], (((1,), (1,)), ((), ())), preferred_element_type=F32)
            fresh = jnp.where(lanes == slot, new_scores[b], -jnp.inf)
            scores[b] = jnp.where(lanes < slot, raw * scale, fresh)

    for c in range(SEQ_CHUNKS):
        score_chunk(c)

    pairs = lax.broadcasted_iota(jnp.int32, (128, block_len), 1)
    half_pairs = group // 2 * repeat
    low = lax.broadcasted_iota(jnp.int32, (1, 128), 1) < half_pairs
    for c in range(rows // group):
        part = slice(c * group, (c + 1) * group)
        s = scores[part].reshape(128, block_len)
        top = jnp.max(s, axis=-1, keepdims=True)
        p = jnp.where(s > -jnp.inf, jnp.exp(s - top), 0.0)
        total = jnp.sum(p, axis=-1, keepdims=True)
        probs[part] = p.reshape(group, repeat, block_len)
        turned = jnp.where(pairs == 0, top, jnp.where(pairs == 1, total, 0.0)).T
        m_row, l_row = turned[0:1], turned[1:2]
        stats_ref[2 * c] = jnp.where(low, m_row, pltpu.roll(l_row, half_pairs, 1))
        stats_ref[2 * c + 1] = jnp.where(low, pltpu.roll(m_row, half_pairs, 1), l_row)

    def mix_chunk(c):
        cache_copy(v_hbm, vbuf, v_sem, c).wait()
        for b in range(c * per, (c + 1) * per):
            here = lanes == lens_ref[b] - base
            p = probs[b].astype(BF16).astype(F32)
            fresh = jnp.sum(jnp.where(here, p, 0.0), axis=-1, keepdims=True)
            mix_ref[b] = dot(jnp.where(here, 0.0, p).astype(BF16), vbuf[b]) + fresh * new_rows[b:b + 1, head_dim:]

    for c in range(SEQ_CHUNKS):
        mix_chunk(c)

    pl.semaphore_wait(barrier, n)
    for peer in peers:
        pltpu.make_async_remote_copy(mix_ref.at[peer], got_mix.at[me], mix_send, mix_recv, device_id={'sp': peer}, device_id_type=MESH).start()
        pltpu.make_async_remote_copy(stats_ref.at[peer // per_row], got_stats.at[me], st_send, st_recv, device_id={'sp': peer}, device_id_type=MESH).start()
    got_mix[me] = mix_ref[me]
    got_stats[me] = stats_ref[me // per_row]

    tile = lax.broadcasted_iota(jnp.int32, (block_len, head_dim), 0)

    def insert(b, carry):
        here = tile == lens_ref[b] - base
        new = new_rows[pl.ds(b, 1), :].astype(BF16)
        kbuf[b] = jnp.where(here, jnp.broadcast_to(new[:, :head_dim], here.shape), kbuf[b])
        vbuf[b] = jnp.where(here, jnp.broadcast_to(new[:, head_dim:], here.shape), vbuf[b])
        return carry

    lax.fori_loop(0, rows, insert, 0)

    def bulk(ref, send, recv):
        span = ref.at[pl.ds(0, n - 1)]
        return pltpu.make_async_remote_copy(span, span, send, recv, device_id={'tp': partner}, device_id_type=MESH)

    bulk(got_stats, st_send, st_recv).wait_recv()
    flipped[...] = got_stats[:, 0, :].T
    first = pl.multiple_of(lax.rem(me, per_row) * repeat, repeat)
    tops = flipped[pl.ds(first, repeat), :]
    totals = flipped[pl.ds(pl.multiple_of(per_row * repeat + first, repeat), repeat), :]
    factor = jnp.exp(tops - jnp.max(tops, axis=-1, keepdims=True))
    total = jnp.sum(factor * totals, axis=-1, keepdims=True)
    bulk(got_mix, mix_send, mix_recv).wait_recv()
    ways = 4
    sums = [factor[:, s:s + 1] * got_mix[s] for s in range(ways)]
    for s in range(ways, n):
        sums[s % ways] = sums[s % ways] + factor[:, s:s + 1] * got_mix[s]
    mixed = (sums[0] + sums[1]) + (sums[2] + sums[3])
    row = (mixed / total).astype(BF16).astype(F32)
    own[...] = row
    gathered[me] = row
    for peer in peers:
        pltpu.make_async_remote_copy(own, gathered.at[me], own_send, own_recv, device_id={'sp': peer}, device_id_type=MESH).start()
    small[3].wait()
    wo_copy.wait()
    bulk(gathered, own_send, own_recv).wait_recv()
    attended = jnp.concatenate([gathered[:, h, :] for h in range(repeat)], axis=-1).astype(BF16)

    def exchange(mine, theirs, send, recv, c):
        return pltpu.make_async_remote_copy(mine.at[c], theirs.at[c], send.at[c], recv.at[c], device_id={'tp': partner}, device_id_type=MESH)

    for c in range(outs):
        sent[c] = dot(attended, wo[:, c * OUT_COLS:(c + 1) * OUT_COLS])
        exchange(sent, other, o_send, o_recv, c).start()
    for c in range(outs):
        exchange(sent, other, o_send, o_recv, c).wait_recv()
        cols = slice(c * OUT_COLS, (c + 1) * OUT_COLS)
        mid_ref[:, cols] = (hidden_ref[:, cols].astype(F32) + (sent[c] + other[c])).astype(BF16)
    normed_ref[0:rows] = rms_norm(mid_ref[...].astype(F32), gain2_ref[...].astype(F32)[None, :])

    def inner_step(slot, start, width):
        normed = normed_ref[...]
        gate = dot(normed, wg[slot, :, :width])[:rows]
        up = dot(normed, wu[slot, :, :width])[:rows]
        act[0:rows, pl.ds(start, width)] = (jax.nn.silu(gate) * up).astype(BF16)

    def ff_step(i, carry):
        for copy in ff_copies(i):
            copy.wait()
        inner_step(lax.rem(i, FF_SLOTS), pl.multiple_of(i * FF_COLS, FF_COLS), FF_COLS)

        @pl.when(i + FF_SLOTS < full)
        def _():
            for copy in ff_copies(i + FF_SLOTS):
                copy.start()

        if tail:
            @pl.when(i + FF_SLOTS == full)
            def _():
                for copy in ff_copies(full, tail):
                    copy.start()
        return carry

    lax.fori_loop(0, full, ff_step, 0)
    if tail:
        for copy in ff_copies(full, tail):
            copy.wait()
        inner_step(full % FF_SLOTS, full * FF_COLS, tail)

    def down_step(c, carry):
        down_copy(c).wait()
        sent2[c] = dot(act[...], wd[c])[:rows]
        exchange(sent2, other2, d_send, d_recv, c).start()
        return carry

    lax.fori_loop(0, outs, down_step, 0)
    for c in range(outs):
        exchange(sent2, other2, d_send, d_recv, c).wait_recv()
        cols = slice(c * OUT_COLS, (c + 1) * OUT_COLS)
        out_ref[:, cols] = (mid_ref[:, cols].astype(F32) + (sent2[c] + other2[c])).astype(BF16)

    bulk(got_mix, mix_send, mix_recv).wait_send()
    bulk(got_stats, st_send, st_recv).wait_send()
    bulk(gathered, own_send, own_recv).wait_send()
    for c in range(outs):
        exchange(sent, other, o_send, o_recv, c).wait_send()
        exchange(sent2, other2, d_send, d_recv, c).wait_send()


def layer(seq_lens, hidden, gain, gain2, w_q, w_k, w_v, k_cache, v_cache, w_o, w_gate, w_up, w_down):
    rows, block_len, head_dim = k_cache.shape
    repeat = w_q.shape[1] // head_dim
    width = w_o.shape[1]
    inner = w_gate.shape[1]
    outs = width // OUT_COLS
    assert w_q.shape[1] == 2 * FF_COLS
    raw = pl.BlockSpec(memory_space=pltpu.HBM)
    whole = pl.BlockSpec(memory_space=pltpu.VMEM)
    dma = pltpu.SemaphoreType.DMA
    heads = (rows, repeat, head_dim)
    return pl.pallas_call(
        layer_kernel,
        name='layer',
        out_shape=(pltpu.VMEM(hidden.shape, BF16), pltpu.VMEM(k_cache.shape, BF16), pltpu.VMEM(v_cache.shape, BF16)),
        in_specs=[raw] * 13,
        out_specs=(whole, whole, whole),
        scratch_shapes=[
            pltpu.SMEM(seq_lens.shape, jnp.int32),
            pltpu.VMEM(hidden.shape, BF16),
            pltpu.VMEM(gain.shape, BF16),
            pltpu.VMEM(gain2.shape, BF16),
            pltpu.VMEM((width, 2 * head_dim), BF16),
            pltpu.VMEM(heads, F32),
            pltpu.VMEM((rows, 2 * head_dim), F32),
            pltpu.VMEM((rows, repeat, block_len), F32),
            pltpu.VMEM((rows, repeat, block_len), F32),
            pltpu.VMEM((rows, repeat, block_len), F32),
            pltpu.VMEM(heads, F32),
            pltpu.VMEM((2 * rows * repeat // 128, 1, 128), F32),
            pltpu.VMEM(heads, F32),
            pltpu.VMEM((rows, 1, 128), F32),
            pltpu.VMEM((128, rows), F32),
            pltpu.VMEM((repeat, head_dim), F32),
            pltpu.VMEM(heads, F32),
            pltpu.VMEM(w_o.shape, BF16),
            pltpu.VMEM((FF_SLOTS, width, FF_COLS), BF16),
            pltpu.VMEM((FF_SLOTS, width, FF_COLS), BF16),
            pltpu.VMEM((outs, inner, OUT_COLS), BF16),
            pltpu.VMEM((outs, rows, OUT_COLS), F32),
            pltpu.VMEM((outs, rows, OUT_COLS), F32),
            pltpu.VMEM((rows, width), BF16),
            pltpu.VMEM((PAD_ROWS, width), BF16),
            pltpu.VMEM((PAD_ROWS, inner), BF16),
            pltpu.VMEM((outs, rows, OUT_COLS), F32),
            pltpu.VMEM((outs, rows, OUT_COLS), F32),
            dma, dma, dma, dma, dma, dma,
            dma((outs,)), dma((outs,)), dma((outs,)), dma((outs,)),
            dma((4,)), dma((2,)), dma((2,)), dma((SEQ_CHUNKS,)), dma((SEQ_CHUNKS,)),
            dma, dma((FF_SLOTS,)), dma((FF_SLOTS,)), dma((outs,)),
        ],
        compiler_params=pltpu.CompilerParams(collective_id=0, has_side_effects=True, vmem_limit_bytes=59 << 20),
    )(*stay(seq_lens, hidden, gain, gain2, w_q, w_k, w_v, k_cache, v_cache, w_o, w_gate, w_up, w_down))


def write_kernel(*refs):
    count = len(refs) // 2
    sems = refs[-1]
    copies = [pltpu.make_async_copy(refs[i], refs[count + i], sems.at[i]) for i in range(count)]
    for copy in copies:
        copy.start()
    for copy in copies:
        copy.wait()


def write(*arrays):
    return pl.pallas_call(
        write_kernel,
        name='write',
        out_shape=tuple(pltpu.HBM(x.shape, x.dtype) for x in arrays),
        in_specs=[pl.BlockSpec(memory_space=pltpu.VMEM)] * len(arrays),
        out_specs=tuple(pl.BlockSpec(memory_space=pltpu.HBM) for _ in arrays),
        scratch_shapes=[pltpu.SemaphoreType.DMA((len(arrays),))],
        compiler_params=pltpu.CompilerParams(vmem_limit_bytes=4 << 20),
    )(*stay(*arrays, space=pltpu.VMEM))


def solution(mesh):
    cache_spec = P('dp', 'tp', 'sp', None)
    row_spec = P('dp', None)
    col_spec = P(None, 'tp')
    inner_spec = P('tp', None)
    gain_spec = P(None)

    def local_step(hidden, seq_lens, k_cache, v_cache, attn_norm, w_q, w_k, w_v, w_o, mlp_norm, w_gate, w_up, w_down):
        shape = k_cache.shape
        flat = (shape[0] * shape[1], shape[2], shape[3])
        parts = layer(seq_lens, hidden, attn_norm, mlp_norm, w_q, w_k, w_v, k_cache.reshape(flat), v_cache.reshape(flat), w_o, w_gate, w_up, w_down)
        hidden_out, k_out, v_out = write(*parts)
        return hidden_out, k_out.reshape(shape), v_out.reshape(shape)

    return jax.shard_map(local_step, mesh=mesh, in_specs=(row_spec, P('dp'), cache_spec, cache_spec, gain_spec, col_spec, col_spec, col_spec, inner_spec, gain_spec, col_spec, col_spec, inner_spec), out_specs=(row_spec, cache_spec, cache_spec), check_vma=False)
```

time: 588 us -> 45.7 us (0.08)
  blocking collectives: 296 us -> 0 us
  waiting for transfers between devices: 225 us -> 0 us
  Pallas kernels: 0 us -> 44.9 us
  matrix products: 40.2 us -> 0 us
  between operations: 14 us -> 0.64 us
  other arithmetic: 8.54 us -> 0 us
    pmax x1 -> x0, blocking collectives: 296 us -> none  [local_step(): global_max = lax.pmax(jnp.max(scores, axis=-1, keepdims=True), 'sp')]
    psum x3 -> x0, waiting for transfers between devices: 225 us -> none  [the longest x1 175 us: local_step(): merged = lax.psum(jnp.concatenate([local_mix, local_sum], axis=-1), 'sp')]
    pallas_call x0 -> x2, Pallas kernels: none -> 44.9 us  [the longest x1 42.8 us: layer(): pl.pallas_call(layer_kernel, name='layer', out_shape=(pltpu.VMEM(hidden.s...]
    dot_general x8 -> x0, matrix products: 40.2 us -> none  [the longest x1 18.9 us: local_step(): down_part = jnp.dot(activated, w_down, preferred_element_type=jnp.float32)]
  transfers between devices with their start and end apart: 3 -> 0, of which waited for: 3 -> 0; matrix products, arithmetic and copies ran while one was open for 0% -> 0% of each run, Pallas kernels for 0% -> 0%
where the time goes in v4:
time: 45.7 us; the launch traced here: 45.6 us
  Pallas kernels  44.9 us (98%)
  between operations  0.64 us (1%)
    pallas_call x1, Pallas kernels, layer(): pl.pallas_call(layer_kernel, name='layer', out_shape=(pltpu.VMEM(hidden.s...  42.8 us
    pallas_call x1, Pallas kernels, write(): pl.pallas_call(write_kernel, name='write', out_shape=tuple((pltpu.HBM(x.s...  2.12 us

profile of v4, /device:TPU:1, one launch (start us, length us, event | category | flops | bytes accessed | tf_op | source)
XLA Modules:
  0.0 45.6 jit_solution(11065853813005108140)
XLA Ops:
  0.6 42.8 %layer.1 = (bf16[64,2048]{1,0:T(8,128)(2,1)S(1)}, bf16[64,128,128]{2,1,0:T(8,128)(2,1)S(1)}, bf16[64,128,128]{2,1,0:T(8,128)(2,1)S(1)}) custom-call(s32[64]{0:T(128)} %lens_hbm.1, bf16[64,2048]{1,0:T(8,128)(2,1)} %hidden_hbm.1, bf16[2048]{0:T(1024)(128)(2,1)} %gain_hbm.1, bf16[2048]{0:T(1024)(128)(2,1)} %gain2_hbm.1, bf16[2048,1024]{1,0:T(8,128)(2,1)} %wq_hbm.1, ...), custom_call_target="tpu_custom_call" | custom-call | tf_op jit(solution)/shard_map/layer/pallas_call | solution.py:289
  43.5 2.1 %write.1 = (bf16[64,2048]{1,0:T(8,128)(2,1)}, bf16[64,128,128]{2,1,0:T(8,128)(2,1)}, bf16[64,128,128]{2,1,0:T(8,128)(2,1)}) custom-call(bf16[64,2048]{1,0:T(8,128)(2,1)S(1)} %get-tuple-element.9.refs_0_, bf16[64,128,128]{2,1,0:T(8,128)(2,1)S(1)} %get-tuple-element.10.refs_1_, bf16[64,128,128]{2,1,0:T(8,128)(2,1)S(1)} %get-tuple-element.11.refs_2_), custom_call_target="tpu_custom_call" | custom-call | tf_op jit(solution)/shard_map/write/pallas_call | solution.py:344

commit v5 on v4

--- a/solution.py
+++ b/solution.py
@@ -14,8 +14,9 @@
 SEQ_CHUNKS = 4
 PAD_ROWS = 128
 FF_COLS = 512
-FF_SLOTS = 6
+FF_SLOTS = 7
 OUT_COLS = 512
+FF_GROUPS = ((0, 6), (6, 8), (8, 10), (10, 11))
 
 
 def rms_norm(wide, gain):
@@ -33,8 +34,8 @@
 
 def layer_kernel(lens_hbm, hidden_hbm, gain_hbm, gain2_hbm, wq_hbm, wk_hbm, wv_hbm, k_hbm, v_hbm, wo_hbm, wg_hbm, wu_hbm, wd_hbm,
                  out_ref, kbuf, vbuf,
-                 lens_ref, hidden_ref, gain_ref, gain2_ref, wkv, query, new_rows, new_scores, scores, probs, mix_ref, stats_ref,
-                 got_mix, got_stats, flipped, own, gathered, wo, wg, wu, wd, sent, other, mid_ref, normed_ref, act, sent2, other2,
+                 lens_ref, hidden_ref, gain_ref, gain2_ref, query, new_rows, new_scores, scores, probs, mix_ref, stats_ref,
+                 got_mix, got_stats, flipped, own, gathered, wg, wu, wd, sent, other, mid_ref, normed_ref, act, sent2, other2,
                  mix_send, mix_recv, st_send, st_recv, own_send, own_recv, o_send, o_recv, d_send, d_recv,
                  small_sem, w_sem, q_sem, k_sem, v_sem, wo_sem, g_sem, u_sem, wd_sem):
     rows, block_len, head_dim = kbuf.shape
@@ -56,11 +57,12 @@
     for copy in small:
         copy.start()
 
-    kv_copies = [pltpu.make_async_copy(src, wkv.at[:, pl.ds(i * head_dim, head_dim)], w_sem.at[i]) for i, src in enumerate((wk_hbm, wv_hbm))]
+    wkv = wd.at[outs - 1, pl.ds(0, wk_hbm.shape[0]), pl.ds(0, 2 * head_dim)]
+    kv_copies = [pltpu.make_async_copy(src, wd.at[outs - 1, pl.ds(0, wk_hbm.shape[0])].at[:, pl.ds(i * head_dim, head_dim)], w_sem.at[i]) for i, src in enumerate((wk_hbm, wv_hbm))]
     for copy in kv_copies:
         copy.start()
-    last = FF_SLOTS - 1
-    halves = (wg.at[last], wu.at[last])
+    q_slot, o_slot = FF_SLOTS - 2, FF_SLOTS - 1
+    halves = (wg.at[q_slot], wu.at[q_slot])
     q_copies = [pltpu.make_async_copy(wq_hbm.at[:, pl.ds(i * FF_COLS, FF_COLS)], half, q_sem.at[i]) for i, half in enumerate(halves)]
     for copy in q_copies:
         copy.start()
@@ -86,43 +88,46 @@
         pl.semaphore_signal(barrier, inc=1, device_id={'sp': peer}, device_id_type=MESH)
     pl.semaphore_signal(barrier, inc=1, device_id={'tp': partner}, device_id_type=MESH)
 
-    wo_copy = pltpu.make_async_copy(wo_hbm, wo, wo_sem)
-    wo_copy.start()
-
-    def ff_copies(i, width=FF_COLS):
-        slot = lax.rem(i, FF_SLOTS) if not isinstance(i, int) else i % FF_SLOTS
-        start = i * FF_COLS if isinstance(i, int) else pl.multiple_of(i * FF_COLS, FF_COLS)
-        cols = pl.ds(start, width)
+    depth = wo_hbm.shape[0]
+    o_parts = [(wg, wu)[c // 2].at[o_slot, pl.ds(c % 2 * depth, depth)] for c in range(outs)]
+    o_copies = [pltpu.make_async_copy(wo_hbm.at[:, pl.ds(c * OUT_COLS, OUT_COLS)], part, wo_sem.at[c]) for c, part in enumerate(o_parts)]
+
+    chunks = full + (tail > 0)
+
+    def ff_copies(i):
+        slot, width = i % FF_SLOTS, min(FF_COLS, inner - i * FF_COLS)
+        cols = pl.ds(i * FF_COLS, width)
         return (
             pltpu.make_async_copy(wg_hbm.at[:, cols], wg.at[slot, :, pl.ds(0, width)], g_sem.at[slot]),
             pltpu.make_async_copy(wu_hbm.at[:, cols], wu.at[slot, :, pl.ds(0, width)], u_sem.at[slot]),
         )
 
     def down_copy(c):
-        return pltpu.make_async_copy(wd_hbm.at[:, pl.ds(pl.multiple_of(c * OUT_COLS, OUT_COLS), OUT_COLS)], wd.at[c], wd_sem.at[c])
-
-    for i in range(last):
-        for copy in ff_copies(i):
+        return pltpu.make_async_copy(wd_hbm.at[:, pl.ds(c * OUT_COLS, OUT_COLS)], wd.at[c], wd_sem.at[c])
+
+    def start(copies):
+        for copy in copies:
             copy.start()
+
+    def wait(copies):
+        for copy in copies:
+            copy.wait()
 
     normed_ref[rows:] = jnp.zeros((PAD_ROWS - rows, normed_ref.shape[1]), BF16)
     act[rows:] = jnp.zeros((PAD_ROWS - rows, act.shape[1]), BF16)
     for copy in small[:3]:
         copy.wait()
     normed_ref[0:rows] = rms_norm(hidden_ref[...].astype(F32), gain_ref[...].astype(F32)[None, :])
-    for copy in kv_copies:
-        copy.wait()
+    wait(kv_copies)
+    wait(q_copies)
     new_rows[...] = dot(normed_ref[...], wkv[...])[:rows].astype(BF16).astype(F32)
     per_half = FF_COLS // head_dim
     for i, half in enumerate(halves):
-        q_copies[i].wait()
         part = dot(normed_ref[...], half[...])[:rows].astype(BF16).astype(F32)
         for h in range(per_half):
             query[:, i * per_half + h, :] = part[:, h * head_dim:(h + 1) * head_dim]
-    for copy in ff_copies(last):
-        copy.start()
-    for c in range(outs):
-        down_copy(c).start()
+    for i in range(q_slot + 1):
+        start(ff_copies(i))
 
     group = 128 // repeat
     for c in range(rows // group):
@@ -133,13 +138,14 @@
     lanes = lax.broadcasted_iota(jnp.int32, (repeat, block_len), 1)
 
     def score_chunk(c):
-        cache_copy(k_hbm, kbuf, k_sem, c).wait()
         for b in range(c * per, (c + 1) * per):
             slot = lens_ref[b] - base
             raw = lax.dot_general(query[b].astype(BF16), kbuf[b], (((1,), (1,)), ((), ())), preferred_element_type=F32)
             fresh = jnp.where(lanes == slot, new_scores[b], -jnp.inf)
             scores[b] = jnp.where(lanes < slot, raw * scale, fresh)
 
+    wait([cache_copy(k_hbm, kbuf, k_sem, c) for c in range(SEQ_CHUNKS)])
+    wait([cache_copy(v_hbm, vbuf, v_sem, c) for c in range(SEQ_CHUNKS)])
     for c in range(SEQ_CHUNKS):
         score_chunk(c)
 
@@ -159,7 +165,6 @@
         stats_ref[2 * c + 1] = jnp.where(low, pltpu.roll(m_row, half_pairs, 1), l_row)
 
     def mix_chunk(c):
-        cache_copy(v_hbm, vbuf, v_sem, c).wait()
         for b in range(c * per, (c + 1) * per):
             here = lanes == lens_ref[b] - base
             p = probs[b].astype(BF16).astype(F32)
@@ -175,6 +180,8 @@
         pltpu.make_async_remote_copy(stats_ref.at[peer // per_row], got_stats.at[me], st_send, st_recv, device_id={'sp': peer}, device_id_type=MESH).start()
     got_mix[me] = mix_ref[me]
     got_stats[me] = stats_ref[me // per_row]
+    start(o_copies)
+    start([down_copy(c) for c in range(outs)])
 
     tile = lax.broadcasted_iota(jnp.int32, (block_len, head_dim), 0)
 
@@ -210,58 +217,43 @@
     for peer in peers:
         pltpu.make_async_remote_copy(own, gathered.at[me], own_send, own_recv, device_id={'sp': peer}, device_id_type=MESH).start()
     small[3].wait()
-    wo_copy.wait()
+    wait(o_copies)
     bulk(gathered, own_send, own_recv).wait_recv()
     attended = jnp.concatenate([gathered[:, h, :] for h in range(repeat)], axis=-1).astype(BF16)
+    attended = jnp.concatenate([attended, jnp.zeros((PAD_ROWS - rows, attended.shape[1]), BF16)], axis=0)
 
     def exchange(mine, theirs, send, recv, c):
         return pltpu.make_async_remote_copy(mine.at[c], theirs.at[c], send.at[c], recv.at[c], device_id={'tp': partner}, device_id_type=MESH)
 
     for c in range(outs):
-        sent[c] = dot(attended, wo[:, c * OUT_COLS:(c + 1) * OUT_COLS])
+        sent[c] = dot(attended, o_parts[c][...])[:rows]
         exchange(sent, other, o_send, o_recv, c).start()
+    for i in range(o_slot, FF_SLOTS):
+        start(ff_copies(i))
     for c in range(outs):
         exchange(sent, other, o_send, o_recv, c).wait_recv()
         cols = slice(c * OUT_COLS, (c + 1) * OUT_COLS)
         mid_ref[:, cols] = (hidden_ref[:, cols].astype(F32) + (sent[c] + other[c])).astype(BF16)
     normed_ref[0:rows] = rms_norm(mid_ref[...].astype(F32), gain2_ref[...].astype(F32)[None, :])
 
-    def inner_step(slot, start, width):
-        normed = normed_ref[...]
-        gate = dot(normed, wg[slot, :, :width])[:rows]
-        up = dot(normed, wu[slot, :, :width])[:rows]
-        act[0:rows, pl.ds(start, width)] = (jax.nn.silu(gate) * up).astype(BF16)
-
-    def ff_step(i, carry):
-        for copy in ff_copies(i):
-            copy.wait()
-        inner_step(lax.rem(i, FF_SLOTS), pl.multiple_of(i * FF_COLS, FF_COLS), FF_COLS)
-
-        @pl.when(i + FF_SLOTS < full)
-        def _():
-            for copy in ff_copies(i + FF_SLOTS):
-                copy.start()
-
-        if tail:
-            @pl.when(i + FF_SLOTS == full)
-            def _():
-                for copy in ff_copies(full, tail):
-                    copy.start()
-        return carry
-
-    lax.fori_loop(0, full, ff_step, 0)
-    if tail:
-        for copy in ff_copies(full, tail):
-            copy.wait()
-        inner_step(full % FF_SLOTS, full * FF_COLS, tail)
-
-    def down_step(c, carry):
-        down_copy(c).wait()
+    def inner_step(i):
+        slot, width = i % FF_SLOTS, min(FF_COLS, inner - i * FF_COLS)
+        gate = dot(normed_ref[...], wg[slot, :, :width])[:rows]
+        up = dot(normed_ref[...], wu[slot, :, :width])[:rows]
+        act[0:rows, i * FF_COLS:i * FF_COLS + width] = (jax.nn.silu(gate) * up).astype(BF16)
+        if i + FF_SLOTS < chunks:
+            start(ff_copies(i + FF_SLOTS))
+
+    for lo, hi in FF_GROUPS:
+        for i in range(lo, min(hi, chunks)):
+            wait(ff_copies(i))
+        for i in range(lo, min(hi, chunks)):
+            inner_step(i)
+
+    wait([down_copy(c) for c in range(outs)])
+    for c in range(outs):
         sent2[c] = dot(act[...], wd[c])[:rows]
         exchange(sent2, other2, d_send, d_recv, c).start()
-        return carry
-
-    lax.fori_loop(0, outs, down_step, 0)
     for c in range(outs):
         exchange(sent2, other2, d_send, d_recv, c).wait_recv()
         cols = slice(c * OUT_COLS, (c + 1) * OUT_COLS)
@@ -297,7 +289,6 @@
             pltpu.VMEM(hidden.shape, BF16),
             pltpu.VMEM(gain.shape, BF16),
             pltpu.VMEM(gain2.shape, BF16),
-            pltpu.VMEM((width, 2 * head_dim), BF16),
             pltpu.VMEM(heads, F32),
             pltpu.VMEM((rows, 2 * head_dim), F32),
             pltpu.VMEM((rows, repeat, block_len), F32),
@@ -310,7 +301,6 @@
             pltpu.VMEM((128, rows), F32),
             pltpu.VMEM((repeat, head_dim), F32),
             pltpu.VMEM(heads, F32),
-            pltpu.VMEM(w_o.shape, BF16),
             pltpu.VMEM((FF_SLOTS, width, FF_COLS), BF16),
             pltpu.VMEM((FF_SLOTS, width, FF_COLS), BF16),
             pltpu.VMEM((outs, inner, OUT_COLS), BF16),
@@ -324,7 +314,7 @@
             dma, dma, dma, dma, dma, dma,
             dma((outs,)), dma((outs,)), dma((outs,)), dma((outs,)),
             dma((4,)), dma((2,)), dma((2,)), dma((SEQ_CHUNKS,)), dma((SEQ_CHUNKS,)),
-            dma, dma((FF_SLOTS,)), dma((FF_SLOTS,)), dma((outs,)),
+            dma((outs,)), dma((FF_SLOTS,)), dma((FF_SLOTS,)), dma((outs,)),
         ],
         compiler_params=pltpu.CompilerParams(collective_id=0, has_side_effects=True, vmem_limit_bytes=59 << 20),
     )(*stay(seq_lens, hidden, gain, gain2, w_q, w_k, w_v, k_cache, v_cache, w_o, w_gate, w_up, w_down))

time: 45.7 us -> 44.3 us (0.969)
  Pallas kernels: 44.9 us -> 43.4 us
    pallas_call x1, Pallas kernels: 42.8 us -> 41.3 us  [layer(): pl.pallas_call(layer_kernel, name='layer', out_shape=(pltpu.VMEM(hidden.s...]
where the time goes in v5:
time: 44.3 us; the launch traced here: 44.2 us
  Pallas kernels  43.4 us (98%)
  between operations  0.8 us (2%)
    pallas_call x1, Pallas kernels, layer(): pl.pallas_call(layer_kernel, name='layer', out_shape=(pltpu.VMEM(hidden.s...  41.3 us
    pallas_call x1, Pallas kernels, write(): pl.pallas_call(write_kernel, name='write', out_shape=tuple((pltpu.HBM(x.s...  2.12 us

profile of v5, /device:TPU:1, one launch (start us, length us, event | category | flops | bytes accessed | tf_op | source)
XLA Modules:
  0.0 44.2 jit_solution(16919307081925306945)
XLA Ops:
  0.6 41.3 %layer.1 = (bf16[64,2048]{1,0:T(8,128)(2,1)S(1)}, bf16[64,128,128]{2,1,0:T(8,128)(2,1)S(1)}, bf16[64,128,128]{2,1,0:T(8,128)(2,1)S(1)}) custom-call(s32[64]{0:T(128)} %lens_hbm.1, bf16[64,2048]{1,0:T(8,128)(2,1)} %hidden_hbm.1, bf16[2048]{0:T(1024)(128)(2,1)} %gain_hbm.1, bf16[2048]{0:T(1024)(128)(2,1)} %gain2_hbm.1, bf16[2048,1024]{1,0:T(8,128)(2,1)} %wq_hbm.1, ...), custom_call_target="tpu_custom_call" | custom-call | tf_op jit(solution)/shard_map/layer/pallas_call | solution.py:281
  41.9 2.1 %write.1 = (bf16[64,2048]{1,0:T(8,128)(2,1)}, bf16[64,128,128]{2,1,0:T(8,128)(2,1)}, bf16[64,128,128]{2,1,0:T(8,128)(2,1)}) custom-call(bf16[64,2048]{1,0:T(8,128)(2,1)S(1)} %get-tuple-element.9.refs_0_, bf16[64,128,128]{2,1,0:T(8,128)(2,1)S(1)} %get-tuple-element.10.refs_1_, bf16[64,128,128]{2,1,0:T(8,128)(2,1)S(1)} %get-tuple-element.11.refs_2_), custom_call_target="tpu_custom_call" | custom-call | tf_op jit(solution)/shard_map/write/pallas_call | solution.py:334

commit v6 on v5

--- a/solution.py
+++ b/solution.py
@@ -14,9 +14,10 @@
 SEQ_CHUNKS = 4
 PAD_ROWS = 128
 FF_COLS = 512
-FF_SLOTS = 7
+FF_SLOTS = 8
 OUT_COLS = 512
-FF_GROUPS = ((0, 6), (6, 8), (8, 10), (10, 11))
+FF_GROUPS = ((0, 7), (7, 9), (9, 11))
+LAST_SLOT = 3
 
 
 def rms_norm(wide, gain):
@@ -37,7 +38,7 @@
                  lens_ref, hidden_ref, gain_ref, gain2_ref, query, new_rows, new_scores, scores, probs, mix_ref, stats_ref,
                  got_mix, got_stats, flipped, own, gathered, wg, wu, wd, sent, other, mid_ref, normed_ref, act, sent2, other2,
                  mix_send, mix_recv, st_send, st_recv, own_send, own_recv, o_send, o_recv, d_send, d_recv,
-                 small_sem, w_sem, q_sem, k_sem, v_sem, wo_sem, g_sem, u_sem, wd_sem):
+                 small_sem, w_sem, q_sem, k_sem, v_sem, wo_sem, g_sem, u_sem, wd_sem, last_sem):
     rows, block_len, head_dim = kbuf.shape
     repeat = mix_ref.shape[1]
     n = rows
@@ -57,8 +58,8 @@
     for copy in small:
         copy.start()
 
-    wkv = wd.at[outs - 1, pl.ds(0, wk_hbm.shape[0]), pl.ds(0, 2 * head_dim)]
-    kv_copies = [pltpu.make_async_copy(src, wd.at[outs - 1, pl.ds(0, wk_hbm.shape[0])].at[:, pl.ds(i * head_dim, head_dim)], w_sem.at[i]) for i, src in enumerate((wk_hbm, wv_hbm))]
+    wkv = wd.at[outs - 2, pl.ds(0, wk_hbm.shape[0]), pl.ds(0, 2 * head_dim)]
+    kv_copies = [pltpu.make_async_copy(src, wd.at[outs - 2, pl.ds(0, wk_hbm.shape[0])].at[:, pl.ds(i * head_dim, head_dim)], w_sem.at[i]) for i, src in enumerate((wk_hbm, wv_hbm))]
     for copy in kv_copies:
         copy.start()
     q_slot, o_slot = FF_SLOTS - 2, FF_SLOTS - 1
@@ -70,11 +71,6 @@
     def cache_copy(hbm, buf, sems, c):
         part = pl.ds(c * per, per)
         return pltpu.make_async_copy(hbm.at[part], buf.at[part], sems.at[c])
-
-    for c in range(SEQ_CHUNKS):
-        cache_copy(k_hbm, kbuf, k_sem, c).start()
-    for c in range(SEQ_CHUNKS):
-        cache_copy(v_hbm, vbuf, v_sem, c).start()
 
     barrier = pltpu.get_barrier_semaphore()
     side = round(n ** (1 / 3))
@@ -105,6 +101,13 @@
     def down_copy(c):
         return pltpu.make_async_copy(wd_hbm.at[:, pl.ds(c * OUT_COLS, OUT_COLS)], wd.at[c], wd_sem.at[c])
 
+    spans = [(k, min(wg.shape[1], inner - k)) for k in range(0, inner, wg.shape[1])]
+
+    def last_down(j):
+        first, size = spans[j]
+        cols = pl.ds((outs - 1) * OUT_COLS, OUT_COLS)
+        return [pltpu.make_async_copy(wd_hbm.at[pl.ds(first, size), cols], wg.at[LAST_SLOT + j, pl.ds(0, size)], last_sem.at[j])]
+
     def start(copies):
         for copy in copies:
             copy.start()
@@ -117,10 +120,15 @@
     act[rows:] = jnp.zeros((PAD_ROWS - rows, act.shape[1]), BF16)
     for copy in small[:3]:
         copy.wait()
+    for c in range(SEQ_CHUNKS):
+        cache_copy(k_hbm, kbuf, k_sem, c).start()
+    for c in range(SEQ_CHUNKS):
+        cache_copy(v_hbm, vbuf, v_sem, c).start()
+
     normed_ref[0:rows] = rms_norm(hidden_ref[...].astype(F32), gain_ref[...].astype(F32)[None, :])
     wait(kv_copies)
+    new_rows[...] = dot(normed_ref[...], wkv[...])[:rows].astype(BF16).astype(F32)
     wait(q_copies)
-    new_rows[...] = dot(normed_ref[...], wkv[...])[:rows].astype(BF16).astype(F32)
     per_half = FF_COLS // head_dim
     for i, half in enumerate(halves):
         part = dot(normed_ref[...], half[...])[:rows].astype(BF16).astype(F32)
@@ -181,7 +189,7 @@
     got_mix[me] = mix_ref[me]
     got_stats[me] = stats_ref[me // per_row]
     start(o_copies)
-    start([down_copy(c) for c in range(outs)])
+    start([down_copy(c) for c in range(outs - 1)])
 
     tile = lax.broadcasted_iota(jnp.int32, (block_len, head_dim), 0)
 
@@ -243,6 +251,8 @@
         act[0:rows, i * FF_COLS:i * FF_COLS + width] = (jax.nn.silu(gate) * up).astype(BF16)
         if i + FF_SLOTS < chunks:
             start(ff_copies(i + FF_SLOTS))
+        if 0 <= i - LAST_SLOT < len(spans):
+            start(last_down(i - LAST_SLOT))
 
     for lo, hi in FF_GROUPS:
         for i in range(lo, min(hi, chunks)):
@@ -250,10 +260,15 @@
         for i in range(lo, min(hi, chunks)):
             inner_step(i)
 
-    wait([down_copy(c) for c in range(outs)])
-    for c in range(outs):
+    wait([down_copy(c) for c in range(outs - 1)])
+    for c in range(outs - 1):
         sent2[c] = dot(act[...], wd[c])[:rows]
         exchange(sent2, other2, d_send, d_recv, c).start()
+    for j in range(len(spans)):
+        wait(last_down(j))
+    pieces = [dot(act[:, first:first + size], wg[LAST_SLOT + j, :size])[:rows] for j, (first, size) in enumerate(spans)]
+    sent2[outs - 1] = sum(pieces[1:], pieces[0])
+    exchange(sent2, other2, d_send, d_recv, outs - 1).start()
     for c in range(outs):
         exchange(sent2, other2, d_send, d_recv, c).wait_recv()
         cols = slice(c * OUT_COLS, (c + 1) * OUT_COLS)
@@ -303,7 +318,7 @@
             pltpu.VMEM(heads, F32),
             pltpu.VMEM((FF_SLOTS, width, FF_COLS), BF16),
             pltpu.VMEM((FF_SLOTS, width, FF_COLS), BF16),
-            pltpu.VMEM((outs, inner, OUT_COLS), BF16),
+            pltpu.VMEM((outs - 1, inner, OUT_COLS), BF16),
             pltpu.VMEM((outs, rows, OUT_COLS), F32),
             pltpu.VMEM((outs, rows, OUT_COLS), F32),
             pltpu.VMEM((rows, width), BF16),
@@ -314,7 +329,7 @@
             dma, dma, dma, dma, dma, dma,
             dma((outs,)), dma((outs,)), dma((outs,)), dma((outs,)),
             dma((4,)), dma((2,)), dma((2,)), dma((SEQ_CHUNKS,)), dma((SEQ_CHUNKS,)),
-            dma((outs,)), dma((FF_SLOTS,)), dma((FF_SLOTS,)), dma((outs,)),
+            dma((outs,)), dma((FF_SLOTS,)), dma((FF_SLOTS,)), dma((outs - 1,)), dma((-(-inner // width),)),
         ],
         compiler_params=pltpu.CompilerParams(collective_id=0, has_side_effects=True, vmem_limit_bytes=59 << 20),
     )(*stay(seq_lens, hidden, gain, gain2, w_q, w_k, w_v, k_cache, v_cache, w_o, w_gate, w_up, w_down))

time: 44.3 us -> 42.5 us (0.959)
  Pallas kernels: 43.4 us -> 41.6 us
    pallas_call x1, Pallas kernels: 41.3 us -> 39.5 us  [layer(): pl.pallas_call(layer_kernel, name='layer', out_shape=(pltpu.VMEM(hidden.s...]
where the time goes in v6:
time: 42.5 us; the launch traced here: 42.4 us
  Pallas kernels  41.6 us (98%)
  between operations  0.8 us (2%)
    pallas_call x1, Pallas kernels, layer(): pl.pallas_call(layer_kernel, name='layer', out_shape=(pltpu.VMEM(hidden.s...  39.5 us
    pallas_call x1, Pallas kernels, write(): pl.pallas_call(write_kernel, name='write', out_shape=tuple((pltpu.HBM(x.s...  2.12 us

profile of v6, /device:TPU:1, one launch (start us, length us, event | category | flops | bytes accessed | tf_op | source)
XLA Modules:
  0.0 42.4 jit_solution(15129157914033196949)
XLA Ops:
  0.6 39.5 %layer.1 = (bf16[64,2048]{1,0:T(8,128)(2,1)S(1)}, bf16[64,128,128]{2,1,0:T(8,128)(2,1)S(1)}, bf16[64,128,128]{2,1,0:T(8,128)(2,1)S(1)}) custom-call(s32[64]{0:T(128)} %lens_hbm.1, bf16[64,2048]{1,0:T(8,128)(2,1)} %hidden_hbm.1, bf16[2048]{0:T(1024)(128)(2,1)} %gain_hbm.1, bf16[2048]{0:T(1024)(128)(2,1)} %gain2_hbm.1, bf16[2048,1024]{1,0:T(8,128)(2,1)} %wq_hbm.1, ...), custom_call_target="tpu_custom_call" | custom-call | tf_op jit(solution)/shard_map/layer/pallas_call | solution.py:296
  40.1 2.1 %write.1 = (bf16[64,2048]{1,0:T(8,128)(2,1)}, bf16[64,128,128]{2,1,0:T(8,128)(2,1)}, bf16[64,128,128]{2,1,0:T(8,128)(2,1)}) custom-call(bf16[64,2048]{1,0:T(8,128)(2,1)S(1)} %get-tuple-element.9.refs_0_, bf16[64,128,128]{2,1,0:T(8,128)(2,1)S(1)} %get-tuple-element.10.refs_1_, bf16[64,128,128]{2,1,0:T(8,128)(2,1)S(1)} %get-tuple-element.11.refs_2_), custom_call_target="tpu_custom_call" | custom-call | tf_op jit(solution)/shard_map/write/pallas_call | solution.py:349

commit v7 on v6

--- a/solution.py
+++ b/solution.py
@@ -207,17 +207,20 @@
         return pltpu.make_async_remote_copy(span, span, send, recv, device_id={'tp': partner}, device_id_type=MESH)
 
     bulk(got_stats, st_send, st_recv).wait_recv()
+    spread = new_scores
     flipped[...] = got_stats[:, 0, :].T
     first = pl.multiple_of(lax.rem(me, per_row) * repeat, repeat)
     tops = flipped[pl.ds(first, repeat), :]
     totals = flipped[pl.ds(pl.multiple_of(per_row * repeat + first, repeat), repeat), :]
     factor = jnp.exp(tops - jnp.max(tops, axis=-1, keepdims=True))
     total = jnp.sum(factor * totals, axis=-1, keepdims=True)
+    for s in range(n):
+        spread[s] = jnp.broadcast_to(factor[:, s:s + 1], (repeat, head_dim))
     bulk(got_mix, mix_send, mix_recv).wait_recv()
     ways = 4
-    sums = [factor[:, s:s + 1] * got_mix[s] for s in range(ways)]
+    sums = [spread[s] * got_mix[s] for s in range(ways)]
     for s in range(ways, n):
-        sums[s % ways] = sums[s % ways] + factor[:, s:s + 1] * got_mix[s]
+        sums[s % ways] = sums[s % ways] + spread[s] * got_mix[s]
     mixed = (sums[0] + sums[1]) + (sums[2] + sums[3])
     row = (mixed / total).astype(BF16).astype(F32)
     own[...] = row
@@ -235,14 +238,20 @@
 
     for c in range(outs):
         sent[c] = dot(attended, o_parts[c][...])[:rows]
-        exchange(sent, other, o_send, o_recv, c).start()
+        if c:
+            exchange(sent, other, o_send, o_recv, c - 1).start()
+    exchange(sent, other, o_send, o_recv, outs - 1).start()
     for i in range(o_slot, FF_SLOTS):
         start(ff_copies(i))
+    square = jnp.zeros((rows, 1), F32)
     for c in range(outs):
         exchange(sent, other, o_send, o_recv, c).wait_recv()
         cols = slice(c * OUT_COLS, (c + 1) * OUT_COLS)
-        mid_ref[:, cols] = (hidden_ref[:, cols].astype(F32) + (sent[c] + other[c])).astype(BF16)
-    normed_ref[0:rows] = rms_norm(mid_ref[...].astype(F32), gain2_ref[...].astype(F32)[None, :])
+        mid = (hidden_ref[:, cols].astype(F32) + (sent[c] + other[c])).astype(BF16)
+        mid_ref[:, cols] = mid
+        square = square + jnp.sum(jnp.square(mid.astype(F32)), axis=-1, keepdims=True)
+    shrink = lax.rsqrt(square / mid_ref.shape[1] + NORM_EPS)
+    normed_ref[0:rows] = (mid_ref[...].astype(F32) * shrink * gain2_ref[...].astype(F32)[None, :]).astype(BF16)
 
     def inner_step(i):
         slot, width = i % FF_SLOTS, min(FF_COLS, inner - i * FF_COLS)
@@ -263,7 +272,9 @@
     wait([down_copy(c) for c in range(outs - 1)])
     for c in range(outs - 1):
         sent2[c] = dot(act[...], wd[c])[:rows]
-        exchange(sent2, other2, d_send, d_recv, c).start()
+        if c:
+            exchange(sent2, other2, d_send, d_recv, c - 1).start()
+    exchange(sent2, other2, d_send, d_recv, outs - 2).start()
     for j in range(len(spans)):
         wait(last_down(j))
     pieces = [dot(act[:, first:first + size], wg[LAST_SLOT + j, :size])[:rows] for j, (first, size) in enumerate(spans)]

time: 42.5 us -> 42.4 us (level)
  no operation moved by 1% of the time
where the time goes in v7:
time: 42.4 us; the launch traced here: 42.3 us
  Pallas kernels  41.5 us (98%)
  between operations  0.8 us (2%)
    pallas_call x1, Pallas kernels, layer(): pl.pallas_call(layer_kernel, name='layer', out_shape=(pltpu.VMEM(hidden.s...  39.3 us
    pallas_call x1, Pallas kernels, write(): pl.pallas_call(write_kernel, name='write', out_shape=tuple((pltpu.HBM(x.s...  2.12 us

profile of v7, /device:TPU:1, one launch (start us, length us, event | category | flops | bytes accessed | tf_op | source)
XLA Modules:
  0.0 42.3 jit_solution(16876907895059363300)
XLA Ops:
  0.6 39.3 %layer.1 = (bf16[64,2048]{1,0:T(8,128)(2,1)S(1)}, bf16[64,128,128]{2,1,0:T(8,128)(2,1)S(1)}, bf16[64,128,128]{2,1,0:T(8,128)(2,1)S(1)}) custom-call(s32[64]{0:T(128)} %lens_hbm.1, bf16[64,2048]{1,0:T(8,128)(2,1)} %hidden_hbm.1, bf16[2048]{0:T(1024)(128)(2,1)} %gain_hbm.1, bf16[2048]{0:T(1024)(128)(2,1)} %gain2_hbm.1, bf16[2048,1024]{1,0:T(8,128)(2,1)} %wq_hbm.1, ...), custom_call_target="tpu_custom_call" | custom-call | tf_op jit(solution)/shard_map/layer/pallas_call | solution.py:307
  40.0 2.1 %write.1 = (bf16[64,2048]{1,0:T(8,128)(2,1)}, bf16[64,128,128]{2,1,0:T(8,128)(2,1)}, bf16[64,128,128]{2,1,0:T(8,128)(2,1)}) custom-call(bf16[64,2048]{1,0:T(8,128)(2,1)S(1)} %get-tuple-element.9.refs_0_, bf16[64,128,128]{2,1,0:T(8,128)(2,1)S(1)} %get-tuple-element.10.refs_1_, bf16[64,128,128]{2,1,0:T(8,128)(2,1)S(1)} %get-tuple-element.11.refs_2_), custom_call_target="tpu_custom_call" | custom-call | tf_op jit(solution)/shard_map/write/pallas_call | solution.py:360
